TPU v7x, 256 devices: a whole 4x4x8 slice. The times are simulated.
256 devices in a mesh: area: 32 (over y, x, core), rank: 8 (over z).
Axes of the slice: x: 4, y: 4, z: 8, core: 2. Of those that a mesh axis runs over, the one named last changes fastest.
Arguments:
- initial_bits: int32 [2, 48, 1024], P(None, None, ('area', 'rank')), may hold values from -2147483648 to 2147483646
- membrane: float32 [48, 32768], P(None, ('area', 'rank')), may hold values from -100 to 200
- drive: int32 [32768], P(('area', 'rank')), may hold values from 0 to 47
- leak_shift: int32 [32768], P(('area', 'rank')), may hold values from 2 to 5
- weights: bfloat16 [256, 128, 128, 128], P(('area', 'rank')), may hold values from -3 to 3, as said below
- pre_block: int32 [256, 128], P(('area', 'rank')), may hold values from 0 to 255
- block_mask: int32 [256, 128], P(('area', 'rank')), may hold values 0 or 1
- delay: int32 [256, 128], P(('area', 'rank')), may hold values from 2 to 5
- area_of_block: int32 [256, 1], replicated, may hold values from 0 to 31
Outputs:
- final_membrane: float32 [48, 32768], P(None, ('area', 'rank'))
- area_rates: float32 [10, 32], replicated
Inputs may be any that keep to these rules, and one draw needn't show every extreme that they name: weights hold whole numbers. `area_of_block`: every area holds at least one block.
All inputs are finite; a program needn't handle non-finite values. No bound on the sum of `block_mask` on one device may be relied on, other than what follows from the above.
Results may differ from a plain program's by a relative error of at most 0.0003.
Values sent between devices are 32-bit elements; how exact they have to be, the bound alone decides.
No kernel may reach another device: no remote copies, remote signals or barrier semaphores. Data moves between devices by JAX's collectives and lax.ppermute only.
A program may use at most 128 MiB of HBM per device.

v0:
```python
import jax
import jax.numpy as jnp
from jax import lax
from jax.sharding import Mesh
from jax.sharding import PartitionSpec as P

AREAS = 32
DMIN = 2
NDELAY = 4
STEPS = 10
AREA = ("area_0", "area_1", "area_2")
AREA_RANK = ("area_0", "area_1", "area_2", "rank")


threshold_level = 200.0


def laid_out(pieces, dim):
    pieces = jnp.moveaxis(pieces, 0, dim)
    dims = pieces.shape
    return pieces.reshape(*dims[:dim], dims[dim] * dims[dim + 1], *dims[dim + 2 :])


def from_everyone(shard, axis):
    copies = jnp.broadcast_to(shard, (lax.axis_size(axis), *shard.shape))
    return lax.all_to_all(copies, axis, split_axis=0, concat_axis=0, tiled=True)


def gathered_copies(shard, axis, dim):
    return laid_out(from_everyone(shard, axis), dim)


def by_axis(shard, axes):
    for axis in axes:
        shard = lax.psum(shard, axis)
    return shard


def unpack(packed):
    shifts = jnp.arange(32, dtype=jnp.int32)
    bit_values = jnp.bitwise_and(jnp.right_shift(packed[..., None], shifts), 1)
    return bit_values.reshape(packed.shape[:-1] + (packed.shape[-1] * 32,))


def pack_bits(current_spike_flags):
    trials, width = current_spike_flags.shape
    bit_values = current_spike_flags.astype(jnp.int32).reshape(trials, width // 32, 32)
    rolled_history = jnp.left_shift(bit_values, jnp.arange(32, dtype=jnp.int32))
    return jnp.sum(rolled_history, axis=-1, dtype=jnp.int32)


def collect(packed):
    within = gathered_copies(packed, "rank", 2)
    return gathered_copies(within, AREA, 2)


def on_device(
    initial_bits, membrane, drive, leak_shift, weights, pre_block, block_mask, delay, area_of_block
):
    blk_dev, slots, block = (weights.shape[0], weights.shape[1], weights.shape[2])
    trials, width = membrane.shape
    intervals = STEPS // DMIN
    rows_all = DMIN * trials
    lag_table = (
        delay[:, :, None] - DMIN == jnp.arange(NDELAY, dtype=jnp.int32)[None, None, :]
    ).astype(jnp.float32)
    input_weighting = block_mask.astype(jnp.float32)[:, :, None] * lag_table
    lag_mask = jnp.transpose(input_weighting.astype(jnp.bfloat16), (0, 2, 1))[:, :, None, :, None]
    flat_weights = weights.reshape(blk_dev, slots * block, block)
    buffer = jnp.zeros((STEPS + NDELAY, trials, width), jnp.float32)
    history = initial_bits
    membrane_voltage = jnp.floor(membrane)
    leak_scale = 1.0 / jnp.left_shift(jnp.ones_like(leak_shift), leak_shift).astype(jnp.float32)
    drive_float = drive.astype(jnp.float32)
    fired_steps = []
    kept = []
    for interval in range(intervals):
        gathered = collect(history)
        kept.append(gathered)
        total_blocks = gathered.shape[2] * 32 // block
        source_rows = gathered.reshape(rows_all, total_blocks, block // 32)
        picked = jnp.take(source_rows, pre_block.reshape(blk_dev * slots), axis=1)
        selected = unpack(picked).astype(jnp.bfloat16).reshape(rows_all, blk_dev, slots, block)
        selected = jnp.transpose(selected, (1, 0, 2, 3))[:, None, :, :, :]
        lagged_rows = (selected * lag_mask).reshape(blk_dev, NDELAY * rows_all, slots * block)
        product = jnp.einsum(
            "brx,bxy->bry", lagged_rows, flat_weights, preferred_element_type=jnp.float32
        )
        arrived = product.reshape(blk_dev, NDELAY, DMIN, trials, block)
        arrived = jnp.transpose(arrived, (1, 2, 3, 0, 4)).reshape(NDELAY, DMIN, trials, width)
        first_step = (interval - 1) * DMIN
        for lag_index in range(NDELAY):
            for offset in range(DMIN):
                landing = first_step + offset + DMIN + lag_index
                buffer = buffer.at[landing].add(arrived[lag_index, offset])
        packed_list = []
        for offset in range(DMIN):
            current = buffer[interval * DMIN + offset]
            membrane_voltage = (
                membrane_voltage - jnp.floor(membrane_voltage * leak_scale) + current + drive_float
            )
            current_spike_flags = membrane_voltage >= threshold_level
            membrane_voltage = jnp.where(
                current_spike_flags,
                jnp.zeros_like(membrane_voltage),
                jnp.maximum(membrane_voltage, -threshold_level),
            )
            fired_steps.append(current_spike_flags)
            packed_list.append(pack_bits(current_spike_flags))
        history = jnp.stack(packed_list)
    area_table = (area_of_block == jnp.arange(AREAS, dtype=jnp.int32)[None, :]).astype(jnp.float32)
    sizes_per_area = jnp.sum(area_table, axis=0) * (trials * block)
    own_start = lax.axis_index(AREA_RANK) * blk_dev
    own_table = lax.dynamic_slice_in_dim(area_table, own_start, blk_dev, 0)
    block_totals = jnp.stack(
        [
            jnp.sum(
                current_spike_flags.astype(jnp.float32).reshape(trials, blk_dev, block), axis=(0, 2)
            )
            for current_spike_flags in fired_steps
        ]
    )
    partial_counts = jnp.dot(block_totals, own_table, precision=lax.Precision.HIGHEST)
    counts = by_axis(partial_counts, AREA_RANK)
    return (membrane_voltage, counts / sizes_per_area)


def solution(mesh):
    split = Mesh(
        mesh.devices.reshape(4, 4, 2, mesh.shape["rank"]), ("area_0", "area_1", "area_2", "rank")
    )
    return jax.shard_map(
        on_device,
        mesh=split,
        in_specs=(
            P(None, None, AREA_RANK),
            P(None, AREA_RANK),
            P(AREA_RANK),
            P(AREA_RANK),
            P(AREA_RANK, None, None, None),
            P(AREA_RANK, None),
            P(AREA_RANK, None),
            P(AREA_RANK, None),
            P(),
        ),
        out_specs=(P(None, AREA_RANK), P()),
        check_vma=False,
    )
```

profile of v0, /device:TPU:32, one launch (start us, length us, event | category | flops | bytes accessed | tf_op | source)
XLA Modules:
  0.0 469.6 jit_solution(6175274694056865357)
XLA Ops:
  2.0 8.6 %all-to-all-start = ((s32[8,1,384]{2,1,0:T(1,128)}), s32[8,1,384]{2,1,0:T(1,128)S(1)}, u32[]{:S(2)}, u32[]{:S(2)}) async-start(s32[8,1,384]{2,1,0:T(1,128)} %reshape.1665), calls=%async_computation | async-start | bytes 24576 | tf_op jit(solution)/shard_map/all_to_all | solution.py:26
  14.3 2.7 all-to-all-done
  18.8 2.6 reshape.1667
  21.3 7.5 %all-to-all-start.1 = ((s32[32,1,3072]{2,1,0:T(1,128)}), s32[32,1,3072]{2,1,0:T(1,128)S(1)}, u32[]{:S(2)}, u32[]{:S(2)}) async-start(s32[32,1,3072]{2,1,0:T(1,128)} %reshape.1667), calls=%async_computation.1 | async-start | bytes 786432 | tf_op jit(solution)/shard_map/all_to_all | solution.py:26
  28.9 10.2 %all-to-all-done.1 = s32[32,1,3072]{2,1,0:T(1,128)S(1)} async-done(((s32[32,1,3072]{2,1,0:T(1,128)}), s32[32,1,3072]{2,1,0:T(1,128)S(1)}, u32[]{:S(2)}, u32[]{:S(2)}) %all-to-all-start.1) | async-done | bytes 393248 | tf_op jit(solution)/shard_map/all_to_all | solution.py:26
  44.1 3.8 shift_right_arithmetic.145
  47.9 16.9 %shift_right_arithmetic.146 = s32[2,48,16384]{1,0,2:T(2,128)} reshape(s32[96,128,4,32]{0,3,2,1:T(8,128)} %shift_right_arithmetic.145) | data formatting | bytes 12582912 | tf_op jit(solution)/shard_map/shift_right_arithmetic | solution.py:41
  64.8 20.0 %copy.55 = s32[2,48,16384]{2,1,0:T(8,128)} copy(s32[2,48,16384]{1,0,2:T(2,128)} %shift_right_arithmetic.146) | data formatting | bytes 12582912 | tf_op jit(solution)/shard_map/shift_right_arithmetic | solution.py:41
  84.8 3.7 and_convert_fusion.4
  88.8 3.4 fusion.8
  93.4 10.7 %all_to_all.50 = s32[8,1,384]{2,1,0:T(1,128)S(1)} all-to-all(s32[8,1,384]{2,1,0:T(1,128)S(1)} %reshape.1669), channel_id=1, replica_groups=mesh['area_0'=4,'area_1'=4,'area_2'=2,'rank'=8] {'rank'}, dimensions={0} | all-to-all | bytes 24576 | tf_op jit(solution)/shard_map/all_to_all | solution.py:26
  107.3 14.0 %all_to_all.51 = s32[32,1,3072]{2,1,0:T(1,128)S(1)} all-to-all(s32[32,1,3072]{2,1,0:T(1,128)S(1)} %reshape.1671), channel_id=1, replica_groups=mesh['area_0'=4,'area_1'=4,'area_2'=2,'rank'=8] {'area_0','area_1','area..., dimensions={0} | all-to-all | bytes 786432 | tf_op jit(solution)/shard_map/all_to_all | solution.py:26
  126.4 3.8 shift_right_arithmetic.153
  130.2 16.9 %shift_right_arithmetic.154 = s32[2,48,16384]{1,0,2:T(2,128)} reshape(s32[96,128,4,32]{0,3,2,1:T(8,128)} %shift_right_arithmetic.153) | data formatting | bytes 12582912 | tf_op jit(solution)/shard_map/shift_right_arithmetic | solution.py:41
  147.1 20.0 %copy.60 = s32[2,48,16384]{2,1,0:T(8,128)} copy(s32[2,48,16384]{1,0,2:T(2,128)} %shift_right_arithmetic.154) | data formatting | bytes 12582912 | tf_op jit(solution)/shard_map/shift_right_arithmetic | solution.py:41
  167.1 3.7 and_convert_fusion.3
  171.1 3.4 fusion.6
  175.6 10.1 %all_to_all.52 = s32[8,1,384]{2,1,0:T(1,128)S(1)} all-to-all(s32[8,1,384]{2,1,0:T(1,128)S(1)} %reshape.1673), channel_id=1, replica_groups=mesh['area_0'=4,'area_1'=4,'area_2'=2,'rank'=8] {'rank'}, dimensions={0} | all-to-all | bytes 24576 | tf_op jit(solution)/shard_map/all_to_all | solution.py:26
  188.9 13.8 %all_to_all.53 = s32[32,1,3072]{2,1,0:T(1,128)S(1)} all-to-all(s32[32,1,3072]{2,1,0:T(1,128)S(1)} %reshape.1675), channel_id=1, replica_groups=mesh['area_0'=4,'area_1'=4,'area_2'=2,'rank'=8] {'area_0','area_1','area..., dimensions={0} | all-to-all | bytes 786432 | tf_op jit(solution)/shard_map/all_to_all | solution.py:26
  207.8 3.8 shift_right_arithmetic.156
  211.6 16.9 %shift_right_arithmetic.157 = s32[2,48,16384]{1,0,2:T(2,128)} reshape(s32[96,128,4,32]{0,3,2,1:T(8,128)} %shift_right_arithmetic.156) | data formatting | bytes 12582912 | tf_op jit(solution)/shard_map/shift_right_arithmetic | solution.py:41
  228.5 20.0 %copy.65 = s32[2,48,16384]{2,1,0:T(8,128)} copy(s32[2,48,16384]{1,0,2:T(2,128)} %shift_right_arithmetic.157) | data formatting | bytes 12582912 | tf_op jit(solution)/shard_map/shift_right_arithmetic | solution.py:41
  248.5 3.7 and_convert_fusion.2
  252.5 3.4 fusion.4
  257.7 4.7 all-to-all-start.6
  262.5 6.2 %all-to-all-done.6 = s32[8,1,384]{2,1,0:T(1,128)S(1)} async-done(((s32[8,1,384]{2,1,0:T(1,128)}), s32[8,1,384]{2,1,0:T(1,128)S(1)}, u32[]{:S(2)}, u32[]{:S(2)}) %all-to-all-start.6) | async-done | bytes 12320 | tf_op jit(solution)/shard_map/all_to_all | solution.py:26
  270.0 2.6 reshape.1679
  272.6 4.1 all-to-all-start.7
  276.8 10.1 %all-to-all-done.7 = s32[32,1,3072]{2,1,0:T(1,128)S(1)} async-done(((s32[32,1,3072]{2,1,0:T(1,128)}), s32[32,1,3072]{2,1,0:T(1,128)S(1)}, u32[]{:S(2)}, u32[]{:S(2)}) %all-to-all-start.7) | async-done | bytes 393248 | tf_op jit(solution)/shard_map/all_to_all | solution.py:26
  291.9 3.8 shift_right_arithmetic.159
  295.7 16.9 %shift_right_arithmetic.160 = s32[2,48,16384]{1,0,2:T(2,128)} reshape(s32[96,128,4,32]{0,3,2,1:T(8,128)} %shift_right_arithmetic.159) | data formatting | bytes 12582912 | tf_op jit(solution)/shard_map/shift_right_arithmetic | solution.py:41
  312.6 20.0 %copy.70 = s32[2,48,16384]{2,1,0:T(8,128)} copy(s32[2,48,16384]{1,0,2:T(2,128)} %shift_right_arithmetic.160) | data formatting | bytes 12582912 | tf_op jit(solution)/shard_map/shift_right_arithmetic | solution.py:41
  332.6 3.7 and_convert_fusion.1
  336.6 3.4 fusion.2
  341.8 4.7 %all-to-all-start.8 = ((s32[8,1,384]{2,1,0:T(1,128)}), s32[8,1,384]{2,1,0:T(1,128)S(1)}, u32[]{:S(2)}, u32[]{:S(2)}) async-start(s32[8,1,384]{2,1,0:T(1,128)} %reshape.1681), calls=%async_computation.8 | async-start | bytes 24576 | tf_op jit(solution)/shard_map/all_to_all | solution.py:26
  346.5 6.3 %all-to-all-done.8 = s32[8,1,384]{2,1,0:T(1,128)S(1)} async-done(((s32[8,1,384]{2,1,0:T(1,128)}), s32[8,1,384]{2,1,0:T(1,128)S(1)}, u32[]{:S(2)}, u32[]{:S(2)}) %all-to-all-start.8) | async-done | bytes 12320 | tf_op jit(solution)/shard_map/all_to_all | solution.py:26
  354.1 2.6 reshape.1683
  356.7 4.1 all-to-all-start.9
  363.4 7.7 %all-to-all-done.9 = s32[32,1,3072]{2,1,0:T(1,128)S(1)} async-done(((s32[32,1,3072]{2,1,0:T(1,128)}), s32[32,1,3072]{2,1,0:T(1,128)S(1)}, u32[]{:S(2)}, u32[]{:S(2)}) %all-to-all-start.9) | async-done | bytes 393248 | tf_op jit(solution)/shard_map/all_to_all | solution.py:26
  376.1 3.8 shift_right_arithmetic.162
  379.9 16.9 %shift_right_arithmetic.163 = s32[2,48,16384]{1,0,2:T(2,128)} reshape(s32[96,128,4,32]{0,3,2,1:T(8,128)} %shift_right_arithmetic.162) | data formatting | bytes 12582912 | tf_op jit(solution)/shard_map/shift_right_arithmetic | solution.py:41
  396.8 20.0 %copy.75 = s32[2,48,16384]{2,1,0:T(8,128)} copy(s32[2,48,16384]{1,0,2:T(2,128)} %shift_right_arithmetic.163) | data formatting | bytes 12582912 | tf_op jit(solution)/shard_map/shift_right_arithmetic | solution.py:41
  416.8 3.7 and_convert_fusion
  420.8 3.4 fusion
  426.1 6.3 %stack.91 = f32[10,1]{0,1:T(1,128)S(1)} concatenate(f32[1,1]{0,1:T(1,128)} %bitcast.91, f32[1,1]{0,1:T(1,128)} %bitcast.92, f32[1,1]{0,1:T(1,128)} %bitcast.93, f32[1,1]{0,1:T(1,128)} %bitcast.94, f32[1,1]{0,1:T(1,128)} %bitcast.95, f32[1,1]{0,1:T(1,128)} %bitcast.96, f32[1,1]{0,1:T(1,128)} %bitcast.97, f32[1,1]{0,1:T(1,128)} %bitcast.98, f32[1,1]{0,1:T(1,128)} %bitcast.99, ...), dimensions={0} | concatenate | bytes 80 | tf_op jit(solution)/shard_map/stack | solution.py:115
  432.5 8.6 %psum.28 = f32[10,32]{1,0:T(8,128)S(1)} all-reduce(f32[10,32]{1,0:T(8,128)S(1)} %broadcast_multiply_fusion), channel_id=1, replica_groups=mesh['area_0'=4,'area_1'=4,'area_2'=2,'rank'=8] {'area_0'}, use_global_device_ids=true, to_apply=%region_18.20 | all-reduce | flops 320 | bytes 2560 | tf_op jit(solution)/shard_map/psum | solution.py:35
  441.1 9.0 %psum.29 = f32[10,32]{1,0:T(8,128)S(1)} all-reduce(f32[10,32]{1,0:T(8,128)S(1)} %psum.28), channel_id=1, replica_groups=mesh['area_0'=4,'area_1'=4,'area_2'=2,'rank'=8] {'area_1'}, use_global_device_ids=true, to_apply=%region_19.21 | all-reduce | flops 320 | bytes 2560 | tf_op jit(solution)/shard_map/psum | solution.py:35
  452.7 15.9 %psum.31 = f32[10,32]{1,0:T(8,128)S(1)} all-reduce(f32[10,32]{1,0:T(8,128)S(1)} %psum.30), channel_id=1, replica_groups=mesh['area_0'=4,'area_1'=4,'area_2'=2,'rank'=8] {'rank'}, use_global_device_ids=true, to_apply=%region_21.23 | all-reduce | flops 320 | bytes 2560 | tf_op jit(solution)/shard_map/psum | solution.py:35
  (192 shorter events, 55.4 us)
Async XLA Ops:
  0.6 0.7 copy-start
  2.0 14.9 %all-to-all-start = ((s32[8,1,384]{2,1,0:T(1,128)}), s32[8,1,384]{2,1,0:T(1,128)S(1)}, u32[]{:S(2)}, u32[]{:S(2)}) async-start(s32[8,1,384]{2,1,0:T(1,128)} %reshape.1665), calls=%async_computation | async-start | bytes 24576 | tf_op jit(solution)/shard_map/all_to_all | solution.py:26
  21.3 17.7 %all-to-all-start.1 = ((s32[32,1,3072]{2,1,0:T(1,128)}), s32[32,1,3072]{2,1,0:T(1,128)S(1)}, u32[]{:S(2)}, u32[]{:S(2)}) async-start(s32[32,1,3072]{2,1,0:T(1,128)} %reshape.1667), calls=%async_computation.1 | async-start | bytes 786432 | tf_op jit(solution)/shard_map/all_to_all | solution.py:26
  84.8 4.0 copy-start.4
  88.8 3.6 copy-start.2
  167.1 4.0 copy-start.5
  248.5 4.0 copy-start.6
  252.5 9.9 %copy-start.3 = (s32[256,1]{0,1:T(1,128)S(1)}, s32[256,1]{0,1:T(1,128)}, u32[]{:S(2)}) copy-start(s32[256,1]{0,1:T(1,128)} %param.99) | copy-start | bytes 3076
  257.7 11.0 %all-to-all-start.6 = ((s32[8,1,384]{2,1,0:T(1,128)}), s32[8,1,384]{2,1,0:T(1,128)S(1)}, u32[]{:S(2)}, u32[]{:S(2)}) async-start(s32[8,1,384]{2,1,0:T(1,128)} %reshape.1677), calls=%async_computation.6 | async-start | bytes 24576 | tf_op jit(solution)/shard_map/all_to_all | solution.py:26
  272.6 14.3 %all-to-all-start.7 = ((s32[32,1,3072]{2,1,0:T(1,128)}), s32[32,1,3072]{2,1,0:T(1,128)S(1)}, u32[]{:S(2)}, u32[]{:S(2)}) async-start(s32[32,1,3072]{2,1,0:T(1,128)} %reshape.1679), calls=%async_computation.7 | async-start | bytes 786432 | tf_op jit(solution)/shard_map/all_to_all | solution.py:26
  332.6 4.0 copy-start.7
  341.8 11.1 %all-to-all-start.8 = ((s32[8,1,384]{2,1,0:T(1,128)}), s32[8,1,384]{2,1,0:T(1,128)S(1)}, u32[]{:S(2)}, u32[]{:S(2)}) async-start(s32[8,1,384]{2,1,0:T(1,128)} %reshape.1681), calls=%async_computation.8 | async-start | bytes 24576 | tf_op jit(solution)/shard_map/all_to_all | solution.py:26
  356.7 14.3 %all-to-all-start.9 = ((s32[32,1,3072]{2,1,0:T(1,128)}), s32[32,1,3072]{2,1,0:T(1,128)S(1)}, u32[]{:S(2)}, u32[]{:S(2)}) async-start(s32[32,1,3072]{2,1,0:T(1,128)} %reshape.1683), calls=%async_computation.9 | async-start | bytes 786432 | tf_op jit(solution)/shard_map/all_to_all | solution.py:26
  416.8 4.0 copy-start.8
  420.8 48.3 %copy-start.1 = (s32[2,48,4]{1,2,0:T(4,128)S(1)}, s32[2,48,4]{1,2,0:T(4,128)}, u32[]{:S(2)}) copy-start(s32[2,48,4]{1,2,0:T(4,128)} %param.91) | copy-start | bytes 4612
where the time goes:
time: 478 us; the launch traced here: 470 us
  local copies, waits for them, and re-layouts  246 us (51%)
  blocking collectives  84.7 us (18%)
  waiting for transfers between devices  43.1 us (9%)
  other arithmetic  42.7 us (9%)
  starting transfers between devices  33.7 us (7%)
  matrix products  17 us (4%)
    shift_right_arithmetic x18, local copies, waits for them, and re-layouts, unpack(): bit_values = jnp.bitwise_and(jnp.right_shift(packed[..., None], shifts), 1)  203 us
    all_to_all x4, blocking collectives, from_everyone(): return lax.all_to_all(copies, axis, split_axis=0, concat_axis=0, tiled=True)  48.7 us
    all_to_all x6, waiting for transfers between devices, from_everyone(): return lax.all_to_all(copies, axis, split_axis=0, concat_axis=0, tiled=True)  43.1 us
    psum x4, blocking collectives, by_axis(): shard = lax.psum(shard, axis)  36 us
    all_to_all x6, starting transfers between devices, from_everyone(): return lax.all_to_all(copies, axis, split_axis=0, concat_axis=0, tiled=True)  33.7 us
    unnamed x50, local copies, waits for them, and re-layouts  26.9 us
    convert_element_type x5, other arithmetic, on_device(): unpack(picked).astype(jnp.bfloat16).reshape(rows_all, blk_dev, slots, block)  18.7 us
    dot_general x5, matrix products, on_device(): jnp.einsum('brx,bxy->bry', lagged_rows, flat_weights, preferred_element_t...  17 us
  transfers between devices with their start and end apart: 6, of which 6 were waited for; matrix products, arithmetic and copies ran while one was open for 1% of the time, Pallas kernels for 0%

commit v1 on v0

v1 whole, which is shorter than its diff:
```python
import jax
import jax.numpy as jnp
from jax import lax
from jax.experimental import pallas as pl
from jax.experimental.pallas import tpu as pltpu
from jax.sharding import Mesh
from jax.sharding import PartitionSpec as P

AREAS = 32
DMIN = 2
NDELAY = 4
STEPS = 10
BLOCK = 128
TRIALS = 48
SLOTS = 128
THRESHOLD = 200.0
GROUP = 16
WORDS = 3
HALF = 128 * WORDS
TABLE = 2 * HALF
AREA_RANK = ("area_0", "area_1", "area_2", "rank")
PLANE = ("area_0", "area_1", "rank")

VMEM = pl.BlockSpec(memory_space=pltpu.VMEM)
SMEM = pl.BlockSpec(memory_space=pltpu.SMEM)


def kernel_call(body, outs, ins, scratch, name, limit):
    return pl.pallas_call(
        body,
        out_shape=outs,
        in_specs=ins,
        out_specs=jax.tree.map(lambda _: VMEM, outs),
        scratch_shapes=scratch,
        name=name,
        compiler_params=pltpu.CompilerParams(vmem_limit_bytes=limit << 20),
    )


def row_ids(rows, lanes=BLOCK):
    return lax.broadcasted_iota(jnp.int32, (rows, lanes), 0)


def lane_ids(rows, lanes=BLOCK):
    return lax.broadcasted_iota(jnp.int32, (rows, lanes), 1)


def words_of(spikes):
    words = []
    for j in range(WORDS):
        bits = jnp.zeros((8, BLOCK), jnp.int32)
        for step in range(DMIN):
            for part in range(2):
                shift = row_ids(8) + (8 * part + 16 * step)
                flags = spikes[step][16 * j + 8 * part : 16 * j + 8 * part + 8]
                bits = bits | jnp.where(flags, jnp.left_shift(1, shift), 0)
        words.append(jnp.sum(bits, axis=0, keepdims=True, dtype=jnp.int32))
    return words


def store_copies(out_ref, words):
    which = row_ids(24) % WORDS
    rows = jnp.where(which == 0, words[0], jnp.where(which == 1, words[1], words[2]))
    for copy in range(HALF // 24):
        out_ref[pl.ds(24 * copy, 24), :] = rows


def first_body(bits_ref, out_ref):
    spikes = []
    lane = lane_ids(TRIALS)
    for step in range(DMIN):
        packed = bits_ref[step]
        word = jnp.zeros((TRIALS, BLOCK), jnp.int32)
        for w in range(BLOCK // 32):
            word = jnp.where(lane // 32 == w, packed[:, w : w + 1], word)
        spikes.append(jnp.bitwise_and(jnp.right_shift(word, lane % 32), 1) == 1)
    store_copies(out_ref, words_of(spikes))


def shifted(older, newer):
    return lax.shift_right_logical(older, 16) | jnp.left_shift(newer, 16)


def interval_body(number, n_hist):
    last = number == STEPS // DMIN - 1

    def body(index_ref, *refs):
        hist = refs[: 2 * n_hist]
        w_ref, v_ref, drive_ref, leak_ref, count_ref = refs[2 * n_hist : 2 * n_hist + 5]
        v_out, pk_out, count_out, table, lhs = refs[2 * n_hist + 5 :]

        for half in range(2):
            at = [hist[2 * a + half][...] if a < n_hist else None for a in range(3)]
            for lag in range(NDELAY):
                newer = at[lag // 2]
                if lag % 2:
                    older = at[lag // 2 + 1]
                    if newer is None:
                        rows = None
                    elif older is None:
                        rows = jnp.left_shift(newer, 16)
                    else:
                        rows = shifted(older, newer)
                else:
                    rows = newer
                if rows is None:
                    rows = jnp.zeros((HALF, BLOCK), jnp.int32)
                table[pl.ds(lag * TABLE + half * HALF, HALF), :] = rows
        table[pl.ds(NDELAY * TABLE, 8), :] = jnp.zeros((8, BLOCK), jnp.int32)

        shift = row_ids(32)

        def group(i, acc):
            for k in range(GROUP):
                base = index_ref[0, i * GROUP + k]
                for j in range(WORDS):
                    word = table[pl.ds(base + j, 1), :]
                    bit = jnp.bitwise_and(jnp.right_shift(word, shift), 1)
                    lhs[pl.ds(32 * j, 32), pl.ds(k * BLOCK, BLOCK)] = bit.astype(
                        jnp.float32
                    ).astype(jnp.bfloat16)
            part = w_ref[pl.ds(i * (GROUP * BLOCK), GROUP * BLOCK), :]
            return acc + jnp.dot(lhs[...], part, preferred_element_type=jnp.float32)

        zero = jnp.zeros((DMIN * TRIALS, BLOCK), jnp.float32)
        current = lax.fori_loop(0, SLOTS // GROUP, group, zero)

        v = v_ref[...]
        if number == 0:
            v = jnp.floor(v)
        drive = drive_ref[...].astype(jnp.float32)
        leak = 1.0 / jnp.left_shift(jnp.ones((1, BLOCK), jnp.int32), leak_ref[...]).astype(jnp.float32)
        spikes = []
        for step in range(DMIN):
            arrived = jnp.concatenate(
                [current[32 * j + 16 * step : 32 * j + 16 * step + 16] for j in range(WORDS)], axis=0
            )
            v = v - jnp.floor(v * leak) + arrived + drive
            fired = v >= THRESHOLD
            v = jnp.where(fired, 0.0, jnp.maximum(v, -THRESHOLD))
            spikes.append(fired)
        v_out[...] = v
        if not last:
            store_copies(pk_out, words_of(spikes))
        lane = lane_ids(8)
        counts = count_ref[...] if number else jnp.zeros((8, BLOCK), jnp.float32)
        for step in range(DMIN):
            total = jnp.sum(spikes[step].astype(jnp.float32), axis=0, keepdims=True)
            total = jnp.sum(total, axis=1, keepdims=True)
            counts = counts + jnp.where(lane == number * DMIN + step, total, 0.0)
        count_out[...] = counts
        if last:
            for copy in range(pk_out.shape[0] // 8):
                pk_out[pl.ds(8 * copy, 8), :] = counts

    return body


def rates_body(counts_ref, area_ref, out_ref):
    counts = counts_ref[...]
    table = (area_ref[...] == lane_ids(counts.shape[0])).astype(jnp.float32)
    sizes = jnp.sum(table, axis=0, keepdims=True) * float(TRIALS * BLOCK)
    sums = lax.dot_general(
        counts, table, (((0,), (0,)), ((), ())), precision=lax.Precision.HIGHEST,
        preferred_element_type=jnp.float32,
    )
    out_ref[...] = sums[:STEPS, :AREAS] / sizes[:, :AREAS]


def exchanged(copies, axes):
    rows = copies.shape[0]
    peers = lax.axis_size(axes)
    pieces = copies.reshape(peers, 1, rows // peers * BLOCK)
    return lax.all_to_all(pieces, axes, split_axis=0, concat_axis=0).reshape(rows, BLOCK)


def on_device(
    initial_bits, membrane, drive, leak_shift, weights, pre_block, block_mask, delay, area_of_block
):
    words = jax.ShapeDtypeStruct((HALF, BLOCK), jnp.int32)
    volts = jax.ShapeDtypeStruct((TRIALS, BLOCK), jnp.float32)
    totals = jax.ShapeDtypeStruct((8, BLOCK), jnp.float32)
    blocks = area_of_block.shape[0]

    core = lax.axis_index("area_2")
    ranks = lax.axis_size("rank")
    other = jnp.bitwise_xor(pre_block // ranks % 2, core)
    place = pre_block // (2 * ranks) * ranks + pre_block % ranks
    index = (delay - DMIN) * TABLE + other * HALF + place * WORDS
    index = jnp.where(block_mask == 1, index, NDELAY * TABLE)

    flat = weights.reshape(SLOTS * BLOCK, BLOCK)
    drive = drive.reshape(1, BLOCK)
    leak_shift = leak_shift.reshape(1, BLOCK)
    v = membrane
    counts = jnp.zeros((8, BLOCK), jnp.float32)
    copies = kernel_call(first_body, words, [VMEM], [], "first", 8)(initial_bits)
    hist = []
    for number in range(STEPS // DMIN):
        own = exchanged(copies, PLANE)
        partner = lax.ppermute(own, "area_2", [(0, 1), (1, 0)])
        hist = [(own, partner)] + hist[:2]
        last = number == STEPS // DMIN - 1
        out = jax.ShapeDtypeStruct((blocks, BLOCK), jnp.float32) if last else words
        v, copies, counts = kernel_call(
            interval_body(number, len(hist)),
            (volts, out, totals),
            [SMEM] + [VMEM] * (2 * len(hist) + 5),
            [
                pltpu.VMEM((NDELAY * TABLE + 8, BLOCK), jnp.int32),
                pltpu.VMEM((DMIN * TRIALS, GROUP * BLOCK), jnp.bfloat16),
            ],
            "interval",
            24,
        )(index, *[x for pair in hist for x in pair], flat, v, drive, leak_shift, counts)
    everyone = exchanged(copies, AREA_RANK)
    rates = jax.ShapeDtypeStruct((STEPS, AREAS), jnp.float32)
    rates = kernel_call(rates_body, rates, [VMEM, VMEM], [], "rates", 8)(everyone, area_of_block)
    return v, rates


def solution(mesh):
    split = Mesh(
        mesh.devices.reshape(4, 4, 2, mesh.shape["rank"]), ("area_0", "area_1", "area_2", "rank")
    )
    return jax.shard_map(
        on_device,
        mesh=split,
        in_specs=(
            P(None, None, AREA_RANK),
            P(None, AREA_RANK),
            P(AREA_RANK),
            P(AREA_RANK),
            P(AREA_RANK, None, None, None),
            P(AREA_RANK, None),
            P(AREA_RANK, None),
            P(AREA_RANK, None),
            P(),
        ),
        out_specs=(P(None, AREA_RANK), P()),
        check_vma=False,
    )
```

time: 478 us -> 161 us (0.34); the launches traced: 470 us -> 159 us
  local copies, waits for them, and re-layouts: 246 us -> 5.15 us
  other arithmetic: 42.7 us -> 0.71 us
  Pallas kernels: 0 us -> 19.1 us
  matrix products: 17 us -> 0 us
  starting transfers between devices: 33.7 us -> 21.8 us
  waiting for transfers between devices: 43.1 us -> 32 us
  blocking collectives: 84.7 us -> 79.4 us
    shift_right_arithmetic x18 -> x0, local copies, waits for them, and re-layouts: 203 us -> none  [unpack(): bit_values = jnp.bitwise_and(jnp.right_shift(packed[..., None], shifts), 1)]
    psum x4 -> x0, blocking collectives: 36 us -> none  [by_axis(): shard = lax.psum(shard, axis)]
    all_to_all x4, blocking collectives: 48.7 us -> 79.4 us  [exchanged(): lax.all_to_all(pieces, axes, split_axis=0, concat_axis=0)]
    unnamed x50 -> x14, local copies, waits for them, and re-layouts: 26.9 us -> 5.15 us
    convert_element_type x7 -> x0, other arithmetic: 20.1 us -> none  [the longest x5 18.7 us: on_device(): unpack(picked).astype(jnp.bfloat16).reshape(rows_all, blk_dev, slots, block)]
    pallas_call x0 -> x7, Pallas kernels: none -> 19.1 us  [the longest x5 17.4 us: on_device(): kernel_call(interval_body(number, len(hist)), (volts, out, totals), [SMEM...]
    all_to_all x6 -> x2, waiting for transfers between devices: 43.1 us -> 25.5 us  [exchanged(): lax.all_to_all(pieces, axes, split_axis=0, concat_axis=0)]
    dot_general x5 -> x0, matrix products: 17 us -> none  [on_device(): jnp.einsum('brx,bxy->bry', lagged_rows, flat_weights, preferred_element_t...]
  transfers between devices with their start and end apart: 6 -> 7, of which waited for: 6 -> 7; matrix products, arithmetic and copies ran while one was open for 1% -> 1% of each run, Pallas kernels for 0% -> 0%
where the time goes in v1:
time: 161 us; the launch traced here: 159 us
  blocking collectives  79.4 us (49%)
  waiting for transfers between devices  32 us (20%)
  starting transfers between devices  21.8 us (14%)
  Pallas kernels  19.1 us (12%)
  local copies, waits for them, and re-layouts  5.15 us (3%)
    all_to_all x4, blocking collectives, exchanged(): lax.all_to_all(pieces, axes, split_axis=0, concat_axis=0)  79.4 us
    all_to_all x2, waiting for transfers between devices, exchanged(): lax.all_to_all(pieces, axes, split_axis=0, concat_axis=0)  25.5 us
    all_to_all x2, starting transfers between devices, exchanged(): lax.all_to_all(pieces, axes, split_axis=0, concat_axis=0)  21.7 us
    pallas_call x5, Pallas kernels, on_device(): kernel_call(interval_body(number, len(hist)), (volts, out, totals), [SMEM...  17.4 us
    ppermute x5, waiting for transfers between devices, on_device(): partner = lax.ppermute(own, 'area_2', [(0, 1), (1, 0)])  6.48 us
    unnamed x14, local copies, waits for them, and re-layouts  5.15 us
  transfers between devices with their start and end apart: 7, of which 7 were waited for; matrix products, arithmetic and copies ran while one was open for 1% of the time, Pallas kernels for 0%

profile of v1, /device:TPU:32, one launch (start us, length us, event | category | flops | bytes accessed | tf_op | source)
XLA Modules:
  0.0 158.8 jit_solution(7291246412646341754)
XLA Ops:
  0.6 0.8 copy.13.bits_ref
  1.4 0.8 first.1
  2.2 15.0 %all-to-all-start = ((s32[128,1,384]{2,1,0:T(1,128)}), s32[128,1,384]{2,1,0:T(1,128)S(1)}, u32[]{:S(2)}, u32[]{:S(2)}) async-start(s32[128,1,384]{2,1,0:T(1,128)} %bitcast), calls=%async_computation | async-start | bytes 393216 | tf_op jit(solution)/shard_map/all_to_all | solution.py:174
  17.3 13.1 %all-to-all-done = s32[128,1,384]{2,1,0:T(1,128)S(1)} async-done(((s32[128,1,384]{2,1,0:T(1,128)}), s32[128,1,384]{2,1,0:T(1,128)S(1)}, u32[]{:S(2)}, u32[]{:S(2)}) %all-to-all-start) | async-done | bytes 196640 | tf_op jit(solution)/shard_map/all_to_all | solution.py:174
  30.4 0.0 collective-permute-start
  30.4 0.7 compare_select_fusion.2.index_ref
  31.1 0.7 collective-permute-done.refs_1_.refs_3_.refs_5_
  31.8 0.0 copy-start
  31.8 2.2 %copy-done = bf16[1,128,128,128]{3,2,1,0:T(8,128)(2,1)S(1)} copy-done((bf16[1,128,128,128]{3,2,1,0:T(8,128)(2,1)S(1)}, bf16[1,128,128,128]{3,2,1,0:T(8,128)(2,1)}, u32[]{:S(2)}) %copy-start) | copy-done | bytes 4194328
  34.0 0.0 copy-start.2
  34.0 0.7 copy-done.2
  34.7 0.0 copy-start.3
  34.7 0.7 copy-done.3
  35.4 0.0 copy-start.4
  35.4 0.7 copy-done.4
  36.0 3.2 %interval.5 = (f32[48,128]{1,0:T(8,128)S(1)}, s32[384,128]{1,0:T(8,128)S(1)}, f32[8,128]{1,0:T(8,128)S(1)}) custom-call(s32[1,128]{1,0:T(1,128)S(1)} %compare_select_fusion.2.index_ref, s32[384,128]{1,0:T(8,128)S(1)} %bitcast.23, s32[384,128]{1,0:T(8,128)S(1)} %collective-permute-done.refs_1_.refs_3_.refs_5_, bf16[16384,128]{1,0:T(8,128)(2,1)S(1)} %bitcast.17, ...), custom_call_target="tpu_custom_call" | custom-call | tf_op jit(solution)/shard_map/interval/pallas_call | solution.py:205
  39.2 19.8 %all_to_all.30 = s32[128,1,384]{2,1,0:T(1,128)S(1)} all-to-all(s32[128,1,384]{2,1,0:T(1,128)S(1)} %bitcast.43), channel_id=1, replica_groups=mesh['area_0'=4,'area_1'=4,'area_2'=2,'rank'=8] {'area_0','area_1','rank'}, dimensions={0} | all-to-all | bytes 393216 | tf_op jit(solution)/shard_map/all_to_all | solution.py:174
  59.0 0.0 collective-permute-start.1
  59.0 1.4 collective-permute-done.1.refs_1_.refs_3_.refs_5_
  60.4 3.4 %interval.6 = (f32[48,128]{1,0:T(8,128)S(1)}, s32[384,128]{1,0:T(8,128)S(1)}, f32[8,128]{1,0:T(8,128)S(1)}) custom-call(s32[1,128]{1,0:T(1,128)S(1)} %compare_select_fusion.2.index_ref, s32[384,128]{1,0:T(8,128)S(1)} %bitcast.31, s32[384,128]{1,0:T(8,128)S(1)} %collective-permute-done.1.refs_1_.refs_3_.refs_5_, s32[384,128]{1,0:T(8,128)S(1)} %bitcast.24, ...), custom_call_target="tpu_custom_call" | custom-call | tf_op jit(solution)/shard_map/interval/pallas_call | solution.py:205
  63.8 0.0 copy-start.1
  63.8 20.0 %all_to_all.31 = s32[128,1,384]{2,1,0:T(1,128)S(1)} all-to-all(s32[128,1,384]{2,1,0:T(1,128)S(1)} %bitcast.42), channel_id=1, replica_groups=mesh['area_0'=4,'area_1'=4,'area_2'=2,'rank'=8] {'area_0','area_1','rank'}, dimensions={0} | all-to-all | bytes 393216 | tf_op jit(solution)/shard_map/all_to_all | solution.py:174
  83.8 0.0 collective-permute-start.2
  83.8 1.4 collective-permute-done.2.refs_1_.refs_3_.refs_5_
  85.2 3.4 %interval.7 = (f32[48,128]{1,0:T(8,128)S(1)}, s32[384,128]{1,0:T(8,128)S(1)}, f32[8,128]{1,0:T(8,128)S(1)}) custom-call(s32[1,128]{1,0:T(1,128)S(1)} %compare_select_fusion.2.index_ref, s32[384,128]{1,0:T(8,128)S(1)} %bitcast.27, s32[384,128]{1,0:T(8,128)S(1)} %collective-permute-done.2.refs_1_.refs_3_.refs_5_, s32[384,128]{1,0:T(8,128)S(1)} %bitcast.32, ...), custom_call_target="tpu_custom_call" | custom-call | tf_op jit(solution)/shard_map/interval/pallas_call | solution.py:205
  88.6 19.8 %all_to_all.32 = s32[128,1,384]{2,1,0:T(1,128)S(1)} all-to-all(s32[128,1,384]{2,1,0:T(1,128)S(1)} %bitcast.40), channel_id=1, replica_groups=mesh['area_0'=4,'area_1'=4,'area_2'=2,'rank'=8] {'area_0','area_1','rank'}, dimensions={0} | all-to-all | bytes 393216 | tf_op jit(solution)/shard_map/all_to_all | solution.py:174
  108.4 0.0 collective-permute-start.3
  108.4 1.4 collective-permute-done.3.refs_1_.refs_3_
  109.8 0.0 copy-done.1
  109.8 3.4 %interval.8 = (f32[48,128]{1,0:T(8,128)S(1)}, s32[384,128]{1,0:T(8,128)S(1)}, f32[8,128]{1,0:T(8,128)S(1)}) custom-call(s32[1,128]{1,0:T(1,128)S(1)} %compare_select_fusion.2.index_ref, s32[384,128]{1,0:T(8,128)S(1)} %bitcast.35, s32[384,128]{1,0:T(8,128)S(1)} %collective-permute-done.3.refs_1_.refs_3_, s32[384,128]{1,0:T(8,128)S(1)} %bitcast.28, ...), custom_call_target="tpu_custom_call" | custom-call | tf_op jit(solution)/shard_map/interval/pallas_call | solution.py:205
  113.2 0.0 copy-start.5
  113.2 19.9 %all_to_all.33 = s32[128,1,384]{2,1,0:T(1,128)S(1)} all-to-all(s32[128,1,384]{2,1,0:T(1,128)S(1)} %bitcast.41), channel_id=1, replica_groups=mesh['area_0'=4,'area_1'=4,'area_2'=2,'rank'=8] {'area_0','area_1','rank'}, dimensions={0} | all-to-all | bytes 393216 | tf_op jit(solution)/shard_map/all_to_all | solution.py:174
  133.1 0.0 collective-permute-start.4
  133.1 1.4 collective-permute-done.4.refs_1_
  134.5 4.0 %interval.9 = (f32[48,128]{1,0:T(8,128)}, f32[256,128]{1,0:T(8,128)}, f32[8,128]{1,0:T(8,128)}) custom-call(s32[1,128]{1,0:T(1,128)S(1)} %compare_select_fusion.2.index_ref, s32[384,128]{1,0:T(8,128)S(1)} %bitcast.38, s32[384,128]{1,0:T(8,128)S(1)} %collective-permute-done.4.refs_1_, s32[384,128]{1,0:T(8,128)S(1)} %bitcast.36, ...), custom_call_target="tpu_custom_call" | custom-call | tf_op jit(solution)/shard_map/interval/pallas_call | solution.py:205
  138.6 6.7 %all-to-all-start.5 = ((f32[256,1,128]{2,1,0:T(1,128)}), f32[256,1,128]{2,1,0:T(1,128)S(1)}, u32[]{:S(2)}, u32[]{:S(2)}) async-start(f32[256,1,128]{2,1,0:T(1,128)} %bitcast.14), calls=%async_computation.5 | async-start | bytes 262144 | tf_op jit(solution)/shard_map/all_to_all | solution.py:174
  145.3 0.0 copy-done.5
  145.3 0.1 copy.20.area_ref
  145.5 12.4 %all-to-all-done.5 = f32[256,1,128]{2,1,0:T(1,128)S(1)} async-done(((f32[256,1,128]{2,1,0:T(1,128)}), f32[256,1,128]{2,1,0:T(1,128)S(1)}, u32[]{:S(2)}, u32[]{:S(2)}) %all-to-all-start.5) | async-done | bytes 131104 | tf_op jit(solution)/shard_map/all_to_all | solution.py:174
  157.9 0.9 rates.1
  (1 shorter events, 0.0 us)
Async XLA Ops:
  2.2 28.1 %all-to-all-start = ((s32[128,1,384]{2,1,0:T(1,128)}), s32[128,1,384]{2,1,0:T(1,128)S(1)}, u32[]{:S(2)}, u32[]{:S(2)}) async-start(s32[128,1,384]{2,1,0:T(1,128)} %bitcast), calls=%async_computation | async-start | bytes 393216 | tf_op jit(solution)/shard_map/all_to_all | solution.py:174
  30.4 1.4 collective-permute-start
  31.8 2.2 %copy-start = (bf16[1,128,128,128]{3,2,1,0:T(8,128)(2,1)S(1)}, bf16[1,128,128,128]{3,2,1,0:T(8,128)(2,1)}, u32[]{:S(2)}) copy-start(bf16[1,128,128,128]{3,2,1,0:T(8,128)(2,1)} %param.13) | copy-start | bytes 12582916
  34.0 0.7 copy-start.2
  34.7 0.7 copy-start.3
  35.4 0.7 copy-start.4
  59.0 1.4 collective-permute-start.1
  63.8 46.0 %copy-start.1 = (bf16[1,128,128,128]{3,2,1,0:T(8,128)(2,1)S(1)}, bf16[1,128,128,128]{3,2,1,0:T(8,128)(2,1)}, u32[]{:S(2)}) copy-start(bf16[1,128,128,128]{3,2,1,0:T(8,128)(2,1)} %param.13) | copy-start | bytes 12582916
  83.8 1.4 collective-permute-start.2
  108.4 1.4 collective-permute-start.3
  113.2 32.1 %copy-start.5 = (s32[256,1]{0,1:T(1,128)S(1)}, s32[256,1]{0,1:T(1,128)}, u32[]{:S(2)}) copy-start(s32[256,1]{0,1:T(1,128)} %param.17) | copy-start | bytes 3076
  133.1 1.4 collective-permute-start.4
  138.6 19.3 %all-to-all-start.5 = ((f32[256,1,128]{2,1,0:T(1,128)}), f32[256,1,128]{2,1,0:T(1,128)S(1)}, u32[]{:S(2)}, u32[]{:S(2)}) async-start(f32[256,1,128]{2,1,0:T(1,128)} %bitcast.14), calls=%async_computation.5 | async-start | bytes 262144 | tf_op jit(solution)/shard_map/all_to_all | solution.py:174

commit v2 on v1

v2 whole, which is shorter than its diff:
```python
import jax
import jax.numpy as jnp
from jax import lax
from jax.experimental import pallas as pl
from jax.experimental.pallas import tpu as pltpu
from jax.sharding import Mesh
from jax.sharding import PartitionSpec as P

AREAS = 32
DMIN = 2
NDELAY = 4
STEPS = 10
BLOCK = 128
TRIALS = 48
SLOTS = 128
THRESHOLD = 200.0
GROUP = 16
WORDS = 3
HALF = 128 * WORDS
TABLE = 2 * HALF
AREA_RANK = ("area_0", "area_1", "area_2", "rank")
PLANE = ("area_0", "area_1", "rank")

VMEM = pl.BlockSpec(memory_space=pltpu.VMEM)
SMEM = pl.BlockSpec(memory_space=pltpu.SMEM)
ANY = pl.BlockSpec(memory_space=pl.ANY)


def kernel_call(body, outs, ins, scratch, name, limit):
    return pl.pallas_call(
        body,
        out_shape=outs,
        in_specs=ins,
        out_specs=jax.tree.map(lambda _: VMEM, outs),
        scratch_shapes=scratch,
        name=name,
        compiler_params=pltpu.CompilerParams(vmem_limit_bytes=limit << 20),
    )


def row_ids(rows, lanes=BLOCK):
    return lax.broadcasted_iota(jnp.int32, (rows, lanes), 0)


def lane_ids(rows, lanes=BLOCK):
    return lax.broadcasted_iota(jnp.int32, (rows, lanes), 1)


def words_of(spikes):
    words = []
    for j in range(WORDS):
        bits = jnp.zeros((8, BLOCK), jnp.int32)
        for step in range(DMIN):
            for part in range(2):
                shift = row_ids(8) + (8 * part + 16 * step)
                flags = spikes[step][16 * j + 8 * part : 16 * j + 8 * part + 8]
                bits = bits | jnp.where(flags, jnp.left_shift(1, shift), 0)
        words.append(jnp.sum(bits, axis=0, keepdims=True, dtype=jnp.int32))
    return words


def store_copies(out_ref, words):
    which = row_ids(24) % WORDS
    rows = jnp.where(which == 0, words[0], jnp.where(which == 1, words[1], words[2]))
    for copy in range(HALF // 24):
        out_ref[pl.ds(24 * copy, 24), :] = rows


def first_body(bits_ref, out_ref):
    trial = lane_ids(8, TRIALS)
    which = row_ids(8, TRIALS)
    place = jnp.left_shift(1, trial % 16).astype(jnp.float32)
    places = jnp.where(trial // 16 == which, place, 0.0).astype(jnp.bfloat16)
    packed = jnp.zeros((8, BLOCK), jnp.int32)
    shift = row_ids(32, TRIALS)
    for step in range(DMIN):
        bits = [
            jnp.bitwise_and(jnp.right_shift(bits_ref[step, w : w + 1, :], shift), 1)
            for w in range(BLOCK // 32)
        ]
        bits = jnp.concatenate(bits, axis=0).astype(jnp.float32).astype(jnp.bfloat16)
        half = lax.dot_general(
            places, bits, (((1,), (1,)), ((), ())), preferred_element_type=jnp.float32
        )
        packed = packed | jnp.left_shift(half.astype(jnp.int32), 16 * step)
    store_copies(out_ref, [packed[j : j + 1] for j in range(WORDS)])


def plan_body(ranks, core_ref, pre_ref, mask_ref, delay_ref, after_ref, out_ref):
    pre = pre_ref[...]
    lag = delay_ref[...] - DMIN
    other = jnp.bitwise_xor(pre // ranks % 2, core_ref[0, 0])
    place = pre // (2 * ranks) * ranks + pre % ranks
    base = lag * TABLE + other * HALF + place * WORDS
    code = base * SLOTS + lane_ids(1)
    late = jnp.where((other == 1) & (lag < 2), 1, 0)
    kind = jnp.where(mask_ref[...] == 1, late, 2)

    def column(row):
        return jnp.transpose(jnp.broadcast_to(row, (SLOTS, SLOTS)))

    sub, lane = row_ids(SLOTS), lane_ids(SLOTS)
    kind_col, code_col = column(kind), column(code)
    kind_row = jnp.broadcast_to(kind, (SLOTS, SLOTS))
    before = jnp.where((kind_row == kind_col) & (lane < sub), 1, 0)
    rank_col = jnp.sum(before, axis=1, keepdims=True, dtype=jnp.int32)
    nothing = NDELAY * TABLE * SLOTS
    lane8 = lane_ids(8)
    row8 = row_ids(8)
    out = jnp.zeros((8, SLOTS), jnp.int32)
    for k in range(2):
        hit = (kind_col == k) & (rank_col == lane)
        codes = jnp.sum(jnp.where(hit, code_col - nothing, 0), axis=0, keepdims=True, dtype=jnp.int32)
        count = jnp.sum(jnp.where(kind == k, 1, 0), axis=1, keepdims=True, dtype=jnp.int32)
        out = jnp.where(row8 == k, codes + nothing, out)
        out = jnp.where((row8 == 2) & (lane8 == k), count, out)
    out_ref[...] = out


def shifted(older, newer):
    low = 0 if older is None else lax.shift_right_logical(older, 16)
    return low | jnp.left_shift(newer, 16)


def fill(table, lag, half, newer, older):
    at = pl.ds(lag * TABLE + half * HALF, HALF)
    if newer is None:
        table[at, :] = jnp.zeros((HALF, BLOCK), jnp.int32)
    elif lag % 2:
        table[at, :] = shifted(None if older is None else older[...], newer[...])
    else:
        table[at, :] = newer[...]


def arrivals(plan_ref, kind, table, w_ref):
    table[pl.ds(NDELAY * TABLE, 8), :] = jnp.zeros((8, BLOCK), jnp.int32)
    shift = row_ids(32)

    def group(i, acc):
        left, right = [], []
        for k in range(GROUP):
            code = plan_ref[kind, i * GROUP + k]
            base = jnp.right_shift(code, 7)
            slot = jnp.bitwise_and(code, SLOTS - 1)
            rows = []
            for j in range(WORDS):
                word = table[pl.ds(base + j, 1), :]
                bit = jnp.bitwise_and(jnp.right_shift(word, shift), 1)
                rows.append(bit.astype(jnp.float32).astype(jnp.bfloat16))
            left.append(jnp.concatenate(rows, axis=0))
            right.append(w_ref[pl.ds(pl.multiple_of(slot * BLOCK, BLOCK), BLOCK), :])
        left = jnp.concatenate(left, axis=1)
        right = jnp.concatenate(right, axis=0)
        return acc + jnp.dot(left, right, preferred_element_type=jnp.float32)

    zero = jnp.zeros((DMIN * TRIALS, BLOCK), jnp.float32)
    groups = (plan_ref[2, kind] + (GROUP - 1)) // GROUP
    return lax.fori_loop(0, groups, group, zero)


def early_body(n_hist):
    def body(plan_ref, *refs):
        own = list(refs[:n_hist]) + [None] * (3 - n_hist)
        other = list(refs[n_hist : 2 * n_hist - 1]) + [None] * (3 - n_hist)
        w_ref, out_ref, table = refs[2 * n_hist - 1 :]
        for lag in range(NDELAY):
            a = lag // 2
            fill(table, lag, 0, own[a], own[a + 1] if a < 2 else None)
            if lag >= 2:
                fill(table, lag, 1, other[a - 1], other[a] if a < 2 else None)
        out_ref[...] = arrivals(plan_ref, 0, table, w_ref)

    return body


def late_body(number, n_hist):
    last = number == STEPS // DMIN - 1

    def body(plan_ref, *refs):
        newer = refs[0]
        older = refs[1] if n_hist > 1 else None
        rest = refs[min(n_hist, 2) :]
        w_ref, early_ref, v_ref, drive_ref, leak_ref = rest[:5]
        count_ref = rest[5] if number else None
        v_out, pk_out, count_out, table = rest[-4:]

        for lag in range(2):
            fill(table, lag, 1, newer, older)
        current = early_ref[...] + arrivals(plan_ref, 1, table, w_ref)

        v = v_ref[...]
        if number == 0:
            v = jnp.floor(v)
        drive = drive_ref[...].astype(jnp.float32)
        leak = 1.0 / jnp.left_shift(jnp.ones((1, BLOCK), jnp.int32), leak_ref[...]).astype(jnp.float32)
        spikes = []
        for step in range(DMIN):
            arrived = jnp.concatenate(
                [current[32 * j + 16 * step : 32 * j + 16 * step + 16] for j in range(WORDS)], axis=0
            )
            v = v - jnp.floor(v * leak) + arrived + drive
            fired = v >= THRESHOLD
            v = jnp.where(fired, 0.0, jnp.maximum(v, -THRESHOLD))
            spikes.append(fired)
        v_out[...] = v
        if not last:
            store_copies(pk_out, words_of(spikes))
        counts = count_ref[...] if number else jnp.zeros((16, BLOCK), jnp.float32)
        row = row_ids(16)
        for step in range(DMIN):
            total = jnp.sum(spikes[step].astype(jnp.float32), axis=0, keepdims=True)
            counts = jnp.where(row == number * DMIN + step, total, counts)
        count_out[...] = counts
        if last:
            total = jnp.sum(counts, axis=1, keepdims=True)
            total = jnp.where(row == lane_ids(16), total, 0.0)
            total = jnp.sum(total, axis=0, keepdims=True)
            total = jnp.broadcast_to(total, (8, BLOCK))
            for copy in range(pk_out.shape[0] // 8):
                pk_out[pl.ds(8 * copy, 8), :] = total

    return body


def rates_body(counts_ref, area_ref, out_ref):
    counts = counts_ref[...]
    blocks = counts.shape[0]
    table = (area_ref[...] == row_ids(BLOCK, blocks)).astype(jnp.float32)
    sizes = jnp.sum(table, axis=1, keepdims=True) * float(TRIALS * BLOCK)
    table = table.astype(jnp.bfloat16)
    high = jnp.floor(counts * (1.0 / 128.0))
    low = counts - high * 128.0
    sums = [
        jnp.dot(table, part.astype(jnp.bfloat16), preferred_element_type=jnp.float32)
        for part in (high, low)
    ]
    rates = (sums[0] * 128.0 + sums[1]) / sizes
    out_ref[...] = jnp.transpose(rates)[:STEPS, :AREAS]


def exchanged(copies, axes):
    rows = copies.shape[0]
    peers = lax.axis_size(axes)
    pieces = copies.reshape(peers, 1, rows // peers * BLOCK)
    return lax.all_to_all(pieces, axes, split_axis=0, concat_axis=0).reshape(rows, BLOCK)


def on_device(
    initial_bits, membrane, drive, leak_shift, weights, pre_block, block_mask, delay, area_of_block
):
    words = jax.ShapeDtypeStruct((HALF, BLOCK), jnp.int32)
    volts = jax.ShapeDtypeStruct((TRIALS, BLOCK), jnp.float32)
    totals = jax.ShapeDtypeStruct((16, BLOCK), jnp.float32)
    sums = jax.ShapeDtypeStruct((DMIN * TRIALS, BLOCK), jnp.float32)
    blocks = area_of_block.shape[0]
    table = pltpu.VMEM((NDELAY * TABLE + 8, BLOCK), jnp.int32)
    ranks = lax.axis_size("rank")
    core = lax.axis_index("area_2").astype(jnp.int32).reshape(1, 1)

    flat = weights.reshape(SLOTS * BLOCK, BLOCK)
    drive = drive.reshape(1, BLOCK)
    leak_shift = leak_shift.reshape(1, BLOCK)
    v = membrane
    counts = []
    bits = jnp.transpose(initial_bits, (0, 2, 1))
    copies = kernel_call(first_body, words, [VMEM], [], "first", 8)(bits)
    plan = None
    own, other = [], []
    for number in range(STEPS // DMIN):
        mine = exchanged(copies, PLANE)
        theirs = lax.ppermute(mine, "area_2", [(0, 1), (1, 0)])
        if plan is None:
            plan = kernel_call(
                lambda *refs: plan_body(ranks, *refs),
                jax.ShapeDtypeStruct((8, SLOTS), jnp.int32),
                [SMEM, VMEM, VMEM, VMEM, ANY],
                [],
                "plan",
                8,
            )(core, pre_block, block_mask, delay, mine)
        own = [mine] + own[:2]
        n_hist = len(own)
        early = kernel_call(
            early_body(n_hist), sums, [SMEM] + [VMEM] * (2 * n_hist), [table], "early", 24
        )(plan, *own, *other[: n_hist - 1], flat)
        other = [theirs] + other[:2]
        last = number == STEPS // DMIN - 1
        out = jax.ShapeDtypeStruct((blocks, BLOCK), jnp.float32) if last else words
        rest = [*other[:2], flat, early, v, drive, leak_shift, *counts]
        v, copies, count = kernel_call(
            late_body(number, n_hist),
            (volts, out, totals),
            [SMEM] + [VMEM] * len(rest),
            [table],
            "late",
            24,
        )(plan, *rest)
        counts = [count]
    everyone = exchanged(copies, AREA_RANK)
    rates = jax.ShapeDtypeStruct((STEPS, AREAS), jnp.float32)
    rates = kernel_call(rates_body, rates, [VMEM, VMEM], [], "rates", 8)(
        everyone, area_of_block.reshape(1, blocks)
    )
    return v, rates


def solution(mesh):
    split = Mesh(
        mesh.devices.reshape(4, 4, 2, mesh.shape["rank"]), ("area_0", "area_1", "area_2", "rank")
    )
    return jax.shard_map(
        on_device,
        mesh=split,
        in_specs=(
            P(None, None, AREA_RANK),
            P(None, AREA_RANK),
            P(AREA_RANK),
            P(AREA_RANK),
            P(AREA_RANK, None, None, None),
            P(AREA_RANK, None),
            P(AREA_RANK, None),
            P(AREA_RANK, None),
            P(),
        ),
        out_specs=(P(None, AREA_RANK), P()),
        check_vma=False,
    )
```

time: 161 us -> 154 us (0.957)
  blocking collectives: 79.4 us -> 127 us
  waiting for transfers between devices: 32 us -> 0.01 us
  starting transfers between devices: 21.8 us -> 0.01 us
    all_to_all x4 -> x6, blocking collectives: 79.4 us -> 127 us  [exchanged(): lax.all_to_all(pieces, axes, split_axis=0, concat_axis=0)]
    all_to_all x2 -> x0, waiting for transfers between devices: 25.5 us -> none  [exchanged(): lax.all_to_all(pieces, axes, split_axis=0, concat_axis=0)]
    all_to_all x2 -> x0, starting transfers between devices: 21.7 us -> none  [exchanged(): lax.all_to_all(pieces, axes, split_axis=0, concat_axis=0)]
    ppermute x5, waiting for transfers between devices: 6.48 us -> 0.01 us  [on_device(): theirs = lax.ppermute(mine, 'area_2', [(0, 1), (1, 0)])]
    pallas_call x6 -> x12, Pallas kernels: 18.2 us -> 17.4 us  [the longest x5 10.2 us: on_device(): kernel_call(early_body(n_hist), sums, [SMEM] + [VMEM] * (2 * n_hist), [ta...]
    unnamed x14 -> x20, local copies, waits for them, and re-layouts: 5.15 us -> 4.98 us
  transfers between devices with their start and end apart: 7 -> 5, of which waited for: 7 -> 0; matrix products, arithmetic and copies ran while one was open for 1% -> 0% of each run, Pallas kernels for 0% -> 7%
where the time goes in v2:
time: 154 us; the launch traced here: 151 us
  blocking collectives  127 us (82%)
  Pallas kernels  18.2 us (12%)
  local copies, waits for them, and re-layouts  4.98 us (3%)
    all_to_all x6, blocking collectives, exchanged(): lax.all_to_all(pieces, axes, split_axis=0, concat_axis=0)  127 us
    pallas_call x5, Pallas kernels, on_device(): kernel_call(early_body(n_hist), sums, [SMEM] + [VMEM] * (2 * n_hist), [ta...  10.2 us
    pallas_call x5, Pallas kernels, on_device(): kernel_call(late_body(number, n_hist), (volts, out, totals), [SMEM] + [VM...  6.77 us
    unnamed x20, local copies, waits for them, and re-layouts  4.98 us
  transfers between devices with their start and end apart: 5, of which 0 were waited for; matrix products, arithmetic and copies ran while one was open for 0% of the time, Pallas kernels for 7%

profile of v2, /device:TPU:32, one launch (start us, length us, event | category | flops | bytes accessed | tf_op | source)
XLA Modules:
  0.0 151.5 jit_solution(5821905685620022088)
XLA Ops:
  0.6 0.0 copy-start.4
  0.6 0.0 copy-start.3
  0.7 0.0 copy-start.2
  0.7 0.0 copy-start.5
  0.7 0.7 copy-done.5
  1.4 0.2 first.1
  1.5 27.9 %all_to_all.30 = s32[128,1,384]{2,1,0:T(1,128)S(1)} all-to-all(s32[128,1,384]{2,1,0:T(1,128)S(1)} %bitcast.48), channel_id=1, replica_groups=mesh['area_0'=4,'area_1'=4,'area_2'=2,'rank'=8] {'area_0','area_1','rank'}, dimensions={0} | all-to-all | bytes 393216 | tf_op jit(solution)/shard_map/all_to_all | solution.py:245
  29.4 0.0 collective-permute-start
  29.4 0.0 copy-start.7
  29.5 0.7 copy-done.7
  30.1 0.0 copy-start.8
  30.1 0.7 copy-done.8
  30.8 0.0 copy-start.9
  30.8 0.7 copy-done.9
  31.4 0.2 plan.1.plan_ref
  31.6 0.0 copy-start
  31.6 2.2 %copy-done = bf16[1,128,128,128]{3,2,1,0:T(8,128)(2,1)S(1)} copy-done((bf16[1,128,128,128]{3,2,1,0:T(8,128)(2,1)S(1)}, bf16[1,128,128,128]{3,2,1,0:T(8,128)(2,1)}, u32[]{:S(2)}) %copy-start) | copy-done | bytes 4194328
  33.8 0.0 copy-start.1
  33.8 2.0 %early.5.refs_2_ = f32[96,128]{1,0:T(8,128)S(1)} custom-call(s32[8,128]{1,0:T(8,128)S(1)} %plan.1.plan_ref, s32[384,128]{1,0:T(8,128)S(1)} %bitcast.32, bf16[16384,128]{1,0:T(8,128)(2,1)S(1)} %bitcast.20), custom_call_target="tpu_custom_call" | custom-call | tf_op jit(solution)/shard_map/early/pallas_call | solution.py:283
  35.9 0.0 collective-permute-done.refs_0_.refs_2_.refs_1_.refs_4_
  35.9 0.0 copy-done.4
  35.9 0.0 copy-done.3
  35.9 0.0 copy-done.2
  35.9 0.1 copy-done.1
  36.0 1.2 late.5
  37.2 20.1 %all_to_all.31 = s32[128,1,384]{2,1,0:T(1,128)S(1)} all-to-all(s32[128,1,384]{2,1,0:T(1,128)S(1)} %bitcast.53), channel_id=1, replica_groups=mesh['area_0'=4,'area_1'=4,'area_2'=2,'rank'=8] {'area_0','area_1','rank'}, dimensions={0} | all-to-all | bytes 393216 | tf_op jit(solution)/shard_map/all_to_all | solution.py:245
  57.4 0.0 collective-permute-start.1
  57.4 2.0 %early.6.refs_3_ = f32[96,128]{1,0:T(8,128)S(1)} custom-call(s32[8,128]{1,0:T(8,128)S(1)} %plan.1.plan_ref, s32[384,128]{1,0:T(8,128)S(1)} %bitcast.40, s32[384,128]{1,0:T(8,128)S(1)} %bitcast.33, s32[384,128]{1,0:T(8,128)S(1)} %collective-permute-done.refs_0_.refs_2_.refs_1_.refs_4_, bf16[16384,128]{1,0:T(8,128)(2,1)S(1)} %bitcast.22), custom_call_target="tpu_custom_call" | custom-call | tf_op jit(solution)/shard_map/early/pallas_call | solution.py:283
  59.4 0.0 collective-permute-done.1.refs_0_.refs_3_.refs_1_.refs_4_
  59.4 1.2 late.6
  60.7 20.1 %all_to_all.32 = s32[128,1,384]{2,1,0:T(1,128)S(1)} all-to-all(s32[128,1,384]{2,1,0:T(1,128)S(1)} %bitcast.50), channel_id=1, replica_groups=mesh['area_0'=4,'area_1'=4,'area_2'=2,'rank'=8] {'area_0','area_1','rank'}, dimensions={0} | all-to-all | bytes 393216 | tf_op jit(solution)/shard_map/all_to_all | solution.py:245
  80.8 0.0 collective-permute-start.2
  80.8 2.0 %early.7.refs_3_ = f32[96,128]{1,0:T(8,128)S(1)} custom-call(s32[8,128]{1,0:T(8,128)S(1)} %plan.1.plan_ref, s32[384,128]{1,0:T(8,128)S(1)} %bitcast.36, s32[384,128]{1,0:T(8,128)S(1)} %bitcast.41, s32[384,128]{1,0:T(8,128)S(1)} %bitcast.34, s32[384,128]{1,0:T(8,128)S(1)} %collective-permute-done.1.refs_0_.refs_3_.refs_1_.refs_4_, ...), custom_call_target="tpu_custom_call" | custom-call | tf_op jit(solution)/shard_map/early/pallas_call | solution.py:283
  82.9 0.0 collective-permute-done.2.refs_0_.refs_3_.refs_1_.refs_4_
  82.9 1.2 late.7
  84.1 20.1 %all_to_all.33 = s32[128,1,384]{2,1,0:T(1,128)S(1)} all-to-all(s32[128,1,384]{2,1,0:T(1,128)S(1)} %bitcast.51), channel_id=1, replica_groups=mesh['area_0'=4,'area_1'=4,'area_2'=2,'rank'=8] {'area_0','area_1','rank'}, dimensions={0} | all-to-all | bytes 393216 | tf_op jit(solution)/shard_map/all_to_all | solution.py:245
  104.3 0.0 collective-permute-start.3
  104.3 2.0 %early.8.refs_3_ = f32[96,128]{1,0:T(8,128)S(1)} custom-call(s32[8,128]{1,0:T(8,128)S(1)} %plan.1.plan_ref, s32[384,128]{1,0:T(8,128)S(1)} %bitcast.44, s32[384,128]{1,0:T(8,128)S(1)} %bitcast.37, s32[384,128]{1,0:T(8,128)S(1)} %bitcast.42, s32[384,128]{1,0:T(8,128)S(1)} %collective-permute-done.2.refs_0_.refs_3_.refs_1_.refs_4_, ...), custom_call_target="tpu_custom_call" | custom-call | tf_op jit(solution)/shard_map/early/pallas_call | solution.py:283
  106.3 0.0 collective-permute-done.3.refs_0_.refs_3_.refs_1_
  106.3 1.2 late.8
  107.6 20.1 %all_to_all.34 = s32[128,1,384]{2,1,0:T(1,128)S(1)} all-to-all(s32[128,1,384]{2,1,0:T(1,128)S(1)} %bitcast.52), channel_id=1, replica_groups=mesh['area_0'=4,'area_1'=4,'area_2'=2,'rank'=8] {'area_0','area_1','rank'}, dimensions={0} | all-to-all | bytes 393216 | tf_op jit(solution)/shard_map/all_to_all | solution.py:245
  127.7 0.0 collective-permute-start.4
  127.7 2.1 %early.9.refs_3_ = f32[96,128]{1,0:T(8,128)S(1)} custom-call(s32[8,128]{1,0:T(8,128)S(1)} %plan.1.plan_ref, s32[384,128]{1,0:T(8,128)S(1)} %bitcast.47, s32[384,128]{1,0:T(8,128)S(1)} %bitcast.45, s32[384,128]{1,0:T(8,128)S(1)} %bitcast.38, s32[384,128]{1,0:T(8,128)S(1)} %collective-permute-done.3.refs_0_.refs_3_.refs_1_, ...), custom_call_target="tpu_custom_call" | custom-call | tf_op jit(solution)/shard_map/early/pallas_call | solution.py:283
  129.8 0.0 collective-permute-done.4.refs_0_
  129.8 1.8 %late.9 = (f32[48,128]{1,0:T(8,128)}, f32[256,128]{1,0:T(8,128)S(1)}, f32[16,128]{1,0:T(8,128)}) custom-call(s32[8,128]{1,0:T(8,128)S(1)} %plan.1.plan_ref, s32[384,128]{1,0:T(8,128)S(1)} %collective-permute-done.4.refs_0_, s32[384,128]{1,0:T(8,128)S(1)} %collective-permute-done.3.refs_0_.refs_3_.refs_1_, bf16[16384,128]{1,0:T(8,128)(2,1)S(1)} %bitcast.29, ...), custom_call_target="tpu_custom_call" | custom-call | tf_op jit(solution)/shard_map/late/pallas_call | solution.py:290
  131.6 19.0 %all_to_all.35 = f32[256,1,128]{2,1,0:T(1,128)S(1)} all-to-all(f32[256,1,128]{2,1,0:T(1,128)S(1)} %bitcast.54), channel_id=1, replica_groups=mesh['area_0'=4,'area_1'=4,'area_2'=2,'rank'=8] {'area_0','area_1','area..., dimensions={0} | all-to-all | bytes 262144 | tf_op jit(solution)/shard_map/all_to_all | solution.py:245
  150.6 0.0 copy-done.6
  150.6 0.8 rates.1
  (1 shorter events, 0.0 us)
Async XLA Ops:
  0.6 35.2 %copy-start.4 = (s32[128]{0:T(128)S(1)}, s32[128]{0:T(128)}, u32[]{:S(2)}) copy-start(s32[128]{0:T(128)} %param.12) | copy-start | bytes 1540
  0.6 35.2 %copy-start.3 = (s32[128]{0:T(128)S(1)}, s32[128]{0:T(128)}, u32[]{:S(2)}) copy-start(s32[128]{0:T(128)} %param.11) | copy-start | bytes 1540
  0.7 35.2 %copy-start.2 = (f32[48,128]{1,0:T(8,128)S(1)}, f32[48,128]{1,0:T(8,128)}, u32[]{:S(2)}) copy-start(f32[48,128]{1,0:T(8,128)} %refs_3_.3) | copy-start | bytes 73732
  0.7 0.7 copy-start.5
  29.4 6.4 %collective-permute-start = (s32[384,128]{1,0:T(8,128)S(1)}, s32[384,128]{1,0:T(8,128)S(1)}, u32[]{:S(2)}, u32[]{:S(2)}) collective-permute-start(s32[384,128]{1,0:T(8,128)S(1)} %bitcast.30), channel_id=1, source_target_pairs={{0,8},{8,0},{1,9},{9,1},{2,10},{10,2},{3,11},{11,3},{4,12},{12,4},... | collective-permute-start | bytes 589832 | tf_op jit(solution)/shard_map/ppermute | solution.py:271
  29.4 0.7 copy-start.7
  30.1 0.7 copy-start.8
  30.8 0.7 copy-start.9
  31.6 2.2 %copy-start = (bf16[1,128,128,128]{3,2,1,0:T(8,128)(2,1)S(1)}, bf16[1,128,128,128]{3,2,1,0:T(8,128)(2,1)}, u32[]{:S(2)}) copy-start(bf16[1,128,128,128]{3,2,1,0:T(8,128)(2,1)} %param.13) | copy-start | bytes 12582916
  33.8 2.2 %copy-start.1 = (bf16[1,128,128,128]{3,2,1,0:T(8,128)(2,1)S(1)}, bf16[1,128,128,128]{3,2,1,0:T(8,128)(2,1)}, u32[]{:S(2)}) copy-start(bf16[1,128,128,128]{3,2,1,0:T(8,128)(2,1)} %param.13) | copy-start | bytes 12582916
  57.4 2.0 %collective-permute-start.1 = (s32[384,128]{1,0:T(8,128)S(1)}, s32[384,128]{1,0:T(8,128)S(1)}, u32[]{:S(2)}, u32[]{:S(2)}) collective-permute-start(s32[384,128]{1,0:T(8,128)S(1)} %bitcast.39), channel_id=1, source_target_pairs={{0,8},{8,0},{1,9},{9,1},{2,10},{10,2},{3,11},{11,3},{4,12},{12,4},... | collective-permute-start | bytes 589832 | tf_op jit(solution)/shard_map/ppermute | solution.py:271
  80.8 2.1 %collective-permute-start.2 = (s32[384,128]{1,0:T(8,128)S(1)}, s32[384,128]{1,0:T(8,128)S(1)}, u32[]{:S(2)}, u32[]{:S(2)}) collective-permute-start(s32[384,128]{1,0:T(8,128)S(1)} %bitcast.35), channel_id=1, source_target_pairs={{0,8},{8,0},{1,9},{9,1},{2,10},{10,2},{3,11},{11,3},{4,12},{12,4},... | collective-permute-start | bytes 589832 | tf_op jit(solution)/shard_map/ppermute | solution.py:271
  104.3 2.1 %collective-permute-start.3 = (s32[384,128]{1,0:T(8,128)S(1)}, s32[384,128]{1,0:T(8,128)S(1)}, u32[]{:S(2)}, u32[]{:S(2)}) collective-permute-start(s32[384,128]{1,0:T(8,128)S(1)} %bitcast.43), channel_id=1, source_target_pairs={{0,8},{8,0},{1,9},{9,1},{2,10},{10,2},{3,11},{11,3},{4,12},{12,4},... | collective-permute-start | bytes 589832 | tf_op jit(solution)/shard_map/ppermute | solution.py:271
  127.7 22.9 %copy-start.6 = (s32[256,1]{0,1:T(1,128)S(1)}, s32[256,1]{0,1:T(1,128)}, u32[]{:S(2)}) copy-start(s32[256,1]{0,1:T(1,128)} %param.17) | copy-start | bytes 3076
  127.7 2.1 %collective-permute-start.4 = (s32[384,128]{1,0:T(8,128)S(1)}, s32[384,128]{1,0:T(8,128)S(1)}, u32[]{:S(2)}, u32[]{:S(2)}) collective-permute-start(s32[384,128]{1,0:T(8,128)S(1)} %bitcast.46), channel_id=1, source_target_pairs={{0,8},{8,0},{1,9},{9,1},{2,10},{10,2},{3,11},{11,3},{4,12},{12,4},... | collective-permute-start | bytes 589832 | tf_op jit(solution)/shard_map/ppermute | solution.py:271

commit v3 on v2

--- a/solution.py
+++ b/solution.py
@@ -23,10 +23,9 @@
 
 VMEM = pl.BlockSpec(memory_space=pltpu.VMEM)
 SMEM = pl.BlockSpec(memory_space=pltpu.SMEM)
-ANY = pl.BlockSpec(memory_space=pl.ANY)
-
-
-def kernel_call(body, outs, ins, scratch, name, limit):
+
+
+def kernel_call(body, outs, ins, scratch, name, limit, cost=None):
     return pl.pallas_call(
         body,
         out_shape=outs,
@@ -34,6 +33,7 @@
         out_specs=jax.tree.map(lambda _: VMEM, outs),
         scratch_shapes=scratch,
         name=name,
+        cost_estimate=cost,
         compiler_params=pltpu.CompilerParams(vmem_limit_bytes=limit << 20),
     )
 
@@ -66,7 +66,7 @@
         out_ref[pl.ds(24 * copy, 24), :] = rows
 
 
-def first_body(bits_ref, out_ref):
+def first_body(input_ref, out_ref, early_ref, late_ref):
     trial = lane_ids(8, TRIALS)
     which = row_ids(8, TRIALS)
     place = jnp.left_shift(1, trial % 16).astype(jnp.float32)
@@ -75,7 +75,7 @@
     shift = row_ids(32, TRIALS)
     for step in range(DMIN):
         bits = [
-            jnp.bitwise_and(jnp.right_shift(bits_ref[step, w : w + 1, :], shift), 1)
+            jnp.bitwise_and(jnp.right_shift(input_ref[4 * step + w : 4 * step + w + 1, :TRIALS], shift), 1)
             for w in range(BLOCK // 32)
         ]
         bits = jnp.concatenate(bits, axis=0).astype(jnp.float32).astype(jnp.bfloat16)
@@ -84,17 +84,23 @@
         )
         packed = packed | jnp.left_shift(half.astype(jnp.int32), 16 * step)
     store_copies(out_ref, [packed[j : j + 1] for j in range(WORDS)])
-
-
-def plan_body(ranks, core_ref, pre_ref, mask_ref, delay_ref, after_ref, out_ref):
-    pre = pre_ref[...]
-    lag = delay_ref[...] - DMIN
-    other = jnp.bitwise_xor(pre // ranks % 2, core_ref[0, 0])
+    rows = [input_ref[8 + i : 9 + i, :] for i in range(4)]
+    plan(slot_codes(lax.axis_size("rank"), *rows), (early_ref, late_ref))
+
+
+def slot_codes(ranks, pre, mask, delay, core):
+    lag = delay - DMIN
+    other = jnp.bitwise_xor(pre // ranks % 2, core)
     place = pre // (2 * ranks) * ranks + pre % ranks
     base = lag * TABLE + other * HALF + place * WORDS
-    code = base * SLOTS + lane_ids(1)
     late = jnp.where((other == 1) & (lag < 2), 1, 0)
-    kind = jnp.where(mask_ref[...] == 1, late, 2)
+    kind = jnp.where(mask == 1, late, 2)
+    return kind * (1 << 20) + base * SLOTS + lane_ids(1)
+
+
+def plan(slots, out_refs):
+    kind = jnp.right_shift(slots, 20)
+    code = jnp.bitwise_and(slots, (1 << 20) - 1)
 
     def column(row):
         return jnp.transpose(jnp.broadcast_to(row, (SLOTS, SLOTS)))
@@ -105,16 +111,12 @@
     before = jnp.where((kind_row == kind_col) & (lane < sub), 1, 0)
     rank_col = jnp.sum(before, axis=1, keepdims=True, dtype=jnp.int32)
     nothing = NDELAY * TABLE * SLOTS
-    lane8 = lane_ids(8)
-    row8 = row_ids(8)
-    out = jnp.zeros((8, SLOTS), jnp.int32)
     for k in range(2):
         hit = (kind_col == k) & (rank_col == lane)
         codes = jnp.sum(jnp.where(hit, code_col - nothing, 0), axis=0, keepdims=True, dtype=jnp.int32)
         count = jnp.sum(jnp.where(kind == k, 1, 0), axis=1, keepdims=True, dtype=jnp.int32)
-        out = jnp.where(row8 == k, codes + nothing, out)
-        out = jnp.where((row8 == 2) & (lane8 == k), count, out)
-    out_ref[...] = out
+        codes = codes + nothing + jnp.where(lane_ids(1) == 0, jnp.left_shift(count, 20), 0)
+        out_refs[k][...] = codes
 
 
 def shifted(older, newer):
@@ -132,20 +134,20 @@
         table[at, :] = newer[...]
 
 
-def arrivals(plan_ref, kind, table, w_ref):
+def arrivals(plan_ref, table, w_ref):
     table[pl.ds(NDELAY * TABLE, 8), :] = jnp.zeros((8, BLOCK), jnp.int32)
-    shift = row_ids(32)
+    mask = jnp.left_shift(1, row_ids(32))
 
     def group(i, acc):
         left, right = [], []
         for k in range(GROUP):
-            code = plan_ref[kind, i * GROUP + k]
-            base = jnp.right_shift(code, 7)
+            code = plan_ref[0, i * GROUP + k]
+            base = jnp.bitwise_and(jnp.right_shift(code, 7), (1 << 13) - 1)
             slot = jnp.bitwise_and(code, SLOTS - 1)
             rows = []
             for j in range(WORDS):
                 word = table[pl.ds(base + j, 1), :]
-                bit = jnp.bitwise_and(jnp.right_shift(word, shift), 1)
+                bit = jnp.bitwise_and(word, mask)
                 rows.append(bit.astype(jnp.float32).astype(jnp.bfloat16))
             left.append(jnp.concatenate(rows, axis=0))
             right.append(w_ref[pl.ds(pl.multiple_of(slot * BLOCK, BLOCK), BLOCK), :])
@@ -154,7 +156,7 @@
         return acc + jnp.dot(left, right, preferred_element_type=jnp.float32)
 
     zero = jnp.zeros((DMIN * TRIALS, BLOCK), jnp.float32)
-    groups = (plan_ref[2, kind] + (GROUP - 1)) // GROUP
+    groups = jnp.right_shift(jnp.right_shift(plan_ref[0, 0], 20) + (GROUP - 1), 4)
     return lax.fori_loop(0, groups, group, zero)
 
 
@@ -168,7 +170,7 @@
             fill(table, lag, 0, own[a], own[a + 1] if a < 2 else None)
             if lag >= 2:
                 fill(table, lag, 1, other[a - 1], other[a] if a < 2 else None)
-        out_ref[...] = arrivals(plan_ref, 0, table, w_ref)
+        out_ref[...] = arrivals(plan_ref, table, w_ref)
 
     return body
 
@@ -186,7 +188,10 @@
 
         for lag in range(2):
             fill(table, lag, 1, newer, older)
-        current = early_ref[...] + arrivals(plan_ref, 1, table, w_ref)
+        current = early_ref[...] + arrivals(plan_ref, table, w_ref)
+        bit = row_ids(32)
+        power = jnp.left_shift(1, jnp.maximum(30 - bit, 0)).astype(jnp.float32)
+        scale = jnp.where(bit == 31, -(2.0**-31), power * 2.0**-30)
 
         v = v_ref[...]
         if number == 0:
@@ -196,7 +201,12 @@
         spikes = []
         for step in range(DMIN):
             arrived = jnp.concatenate(
-                [current[32 * j + 16 * step : 32 * j + 16 * step + 16] for j in range(WORDS)], axis=0
+                [
+                    current[32 * j + 16 * step : 32 * j + 16 * step + 16]
+                    * scale[16 * step : 16 * step + 16]
+                    for j in range(WORDS)
+                ],
+                axis=0,
             )
             v = v - jnp.floor(v * leak) + arrived + drive
             fired = v >= THRESHOLD
@@ -222,7 +232,8 @@
     return body
 
 
-def rates_body(counts_ref, area_ref, out_ref):
+def rates_body(counts_ref, area_ref, v_ref, out_ref, v_out):
+    v_out[...] = v_ref[...]
     counts = counts_ref[...]
     blocks = counts.shape[0]
     table = (area_ref[...] == row_ids(BLOCK, blocks)).astype(jnp.float32)
@@ -254,35 +265,36 @@
     sums = jax.ShapeDtypeStruct((DMIN * TRIALS, BLOCK), jnp.float32)
     blocks = area_of_block.shape[0]
     table = pltpu.VMEM((NDELAY * TABLE + 8, BLOCK), jnp.int32)
-    ranks = lax.axis_size("rank")
-    core = lax.axis_index("area_2").astype(jnp.int32).reshape(1, 1)
+    codes = jax.ShapeDtypeStruct((1, SLOTS), jnp.int32)
 
     flat = weights.reshape(SLOTS * BLOCK, BLOCK)
     drive = drive.reshape(1, BLOCK)
     leak_shift = leak_shift.reshape(1, BLOCK)
     v = membrane
     counts = []
-    bits = jnp.transpose(initial_bits, (0, 2, 1))
-    copies = kernel_call(first_body, words, [VMEM], [], "first", 8)(bits)
-    plan = None
+    bits = jnp.transpose(initial_bits, (0, 2, 1)).reshape(8, TRIALS)
+    first_input = jnp.pad(bits, ((0, 8), (0, BLOCK - TRIALS)))
+    core = lax.broadcast(lax.axis_index("area_2"), (1, BLOCK))
+    for row, values in enumerate((pre_block, block_mask, delay, core), 8):
+        first_input = jnp.where(row_ids(16) == row, values, first_input)
+    copies, early_plan, late_plan = kernel_call(
+        first_body,
+        (words, codes, codes),
+        [VMEM],
+        [],
+        "first",
+        8,
+        pl.CostEstimate(flops=10**10, bytes_accessed=1 << 18, transcendentals=0),
+    )(first_input)
     own, other = [], []
     for number in range(STEPS // DMIN):
         mine = exchanged(copies, PLANE)
         theirs = lax.ppermute(mine, "area_2", [(0, 1), (1, 0)])
-        if plan is None:
-            plan = kernel_call(
-                lambda *refs: plan_body(ranks, *refs),
-                jax.ShapeDtypeStruct((8, SLOTS), jnp.int32),
-                [SMEM, VMEM, VMEM, VMEM, ANY],
-                [],
-                "plan",
-                8,
-            )(core, pre_block, block_mask, delay, mine)
         own = [mine] + own[:2]
         n_hist = len(own)
         early = kernel_call(
             early_body(n_hist), sums, [SMEM] + [VMEM] * (2 * n_hist), [table], "early", 24
-        )(plan, *own, *other[: n_hist - 1], flat)
+        )(early_plan, *own, *other[: n_hist - 1], flat)
         other = [theirs] + other[:2]
         last = number == STEPS // DMIN - 1
         out = jax.ShapeDtypeStruct((blocks, BLOCK), jnp.float32) if last else words
@@ -294,12 +306,12 @@
             [table],
             "late",
             24,
-        )(plan, *rest)
+        )(late_plan, *rest)
         counts = [count]
     everyone = exchanged(copies, AREA_RANK)
     rates = jax.ShapeDtypeStruct((STEPS, AREAS), jnp.float32)
-    rates = kernel_call(rates_body, rates, [VMEM, VMEM], [], "rates", 8)(
-        everyone, area_of_block.reshape(1, blocks)
+    rates, v = kernel_call(rates_body, (rates, volts), [VMEM] * 3, [], "rates", 8)(
+        everyone, area_of_block.reshape(1, blocks), v
     )
     return v, rates
 

time: 154 us -> 149 us (0.968)
  local copies, waits for them, and re-layouts: 4.98 us -> 0.03 us
    unnamed x20 -> x10, local copies, waits for them, and re-layouts: 4.98 us -> 0.03 us
where the time goes in v3:
time: 149 us; the launch traced here: 148 us
  blocking collectives  128 us (86%)
  Pallas kernels  17.4 us (12%)
    all_to_all x6, blocking collectives, exchanged(): lax.all_to_all(pieces, axes, split_axis=0, concat_axis=0)  128 us
    pallas_call x5, Pallas kernels, on_device(): kernel_call(early_body(n_hist), sums, [SMEM] + [VMEM] * (2 * n_hist), [ta...  9.89 us
    pallas_call x5, Pallas kernels, on_device(): kernel_call(late_body(number, n_hist), (volts, out, totals), [SMEM] + [VM...  6.44 us
  transfers between devices with their start and end apart: 5, of which 0 were waited for; matrix products, arithmetic and copies ran while one was open for 0% of the time, Pallas kernels for 7%

profile of v3, /device:TPU:32, one launch (start us, length us, event | category | flops | bytes accessed | tf_op | source)
XLA Modules:
  0.0 147.5 jit_solution(17838710006581190849)
XLA Ops:
  0.7 0.8 select_select_fusion.input_ref
  1.5 0.0 copy-start
  1.5 0.2 first.1
  1.7 0.0 copy-start.1
  1.7 0.0 copy-start.2
  1.7 0.0 copy-start.3
  1.7 28.2 %all_to_all.30 = s32[128,1,384]{2,1,0:T(1,128)S(1)} all-to-all(s32[128,1,384]{2,1,0:T(1,128)S(1)} %bitcast.55), channel_id=1, replica_groups=mesh['area_0'=4,'area_1'=4,'area_2'=2,'rank'=8] {'area_0','area_1','rank'}, dimensions={0} | all-to-all | bytes 393216 | tf_op jit(solution)/shard_map/all_to_all | solution.py:256
  29.9 0.0 collective-permute-start
  29.9 0.0 copy-done
  29.9 2.0 %early.5.refs_2_ = f32[96,128]{1,0:T(8,128)S(1)} custom-call(s32[1,128]{1,0:T(1,128)S(1)} %get-tuple-element.23.plan_ref, s32[384,128]{1,0:T(8,128)S(1)} %bitcast.43, bf16[16384,128]{1,0:T(8,128)(2,1)S(1)} %bitcast.24), custom_call_target="tpu_custom_call" | custom-call | tf_op jit(solution)/shard_map/early/pallas_call | solution.py:295
  31.9 0.0 collective-permute-done.refs_0_.refs_2_.refs_1_.refs_4_
  31.9 0.0 copy-done.1
  31.9 0.0 copy-done.2
  31.9 0.0 copy-done.3
  31.9 1.2 late.5
  33.1 20.4 %all_to_all.31 = s32[128,1,384]{2,1,0:T(1,128)S(1)} all-to-all(s32[128,1,384]{2,1,0:T(1,128)S(1)} %bitcast.56), channel_id=1, replica_groups=mesh['area_0'=4,'area_1'=4,'area_2'=2,'rank'=8] {'area_0','area_1','rank'}, dimensions={0} | all-to-all | bytes 393216 | tf_op jit(solution)/shard_map/all_to_all | solution.py:256
  53.5 0.0 collective-permute-start.1
  53.5 2.0 %early.6.refs_3_ = f32[96,128]{1,0:T(8,128)S(1)} custom-call(s32[1,128]{1,0:T(1,128)S(1)} %get-tuple-element.23.plan_ref, s32[384,128]{1,0:T(8,128)S(1)} %bitcast.39, s32[384,128]{1,0:T(8,128)S(1)} %bitcast.44, s32[384,128]{1,0:T(8,128)S(1)} %collective-permute-done.refs_0_.refs_2_.refs_1_.refs_4_, bf16[16384,128]{1,0:T(8,128)(2,1)S(1)} %bitcast.26), custom_call_target="tpu_custom_call" | custom-call | tf_op jit(solution)/shard_map/early/pallas_call | solution.py:295
  55.5 0.0 collective-permute-done.1.refs_0_.refs_3_.refs_1_.refs_4_
  55.5 1.2 late.6
  56.6 20.4 %all_to_all.32 = s32[128,1,384]{2,1,0:T(1,128)S(1)} all-to-all(s32[128,1,384]{2,1,0:T(1,128)S(1)} %bitcast.52), channel_id=1, replica_groups=mesh['area_0'=4,'area_1'=4,'area_2'=2,'rank'=8] {'area_0','area_1','rank'}, dimensions={0} | all-to-all | bytes 393216 | tf_op jit(solution)/shard_map/all_to_all | solution.py:256
  77.0 0.0 collective-permute-start.2
  77.0 2.0 %early.7.refs_3_ = f32[96,128]{1,0:T(8,128)S(1)} custom-call(s32[1,128]{1,0:T(1,128)S(1)} %get-tuple-element.23.plan_ref, s32[384,128]{1,0:T(8,128)S(1)} %bitcast.35, s32[384,128]{1,0:T(8,128)S(1)} %bitcast.40, s32[384,128]{1,0:T(8,128)S(1)} %bitcast.45, s32[384,128]{1,0:T(8,128)S(1)} %collective-permute-done.1.refs_0_.refs_3_.refs_1_.refs_4_, ...), custom_call_target="tpu_custom_call" | custom-call | tf_op jit(solution)/shard_map/early/pallas_call | solution.py:295
  79.0 0.0 collective-permute-done.2.refs_0_.refs_3_.refs_1_.refs_4_
  79.1 1.2 late.7
  80.2 20.4 %all_to_all.33 = s32[128,1,384]{2,1,0:T(1,128)S(1)} all-to-all(s32[128,1,384]{2,1,0:T(1,128)S(1)} %bitcast.53), channel_id=1, replica_groups=mesh['area_0'=4,'area_1'=4,'area_2'=2,'rank'=8] {'area_0','area_1','rank'}, dimensions={0} | all-to-all | bytes 393216 | tf_op jit(solution)/shard_map/all_to_all | solution.py:256
  100.6 0.0 collective-permute-start.3
  100.6 2.0 %early.8.refs_3_ = f32[96,128]{1,0:T(8,128)S(1)} custom-call(s32[1,128]{1,0:T(1,128)S(1)} %get-tuple-element.23.plan_ref, s32[384,128]{1,0:T(8,128)S(1)} %bitcast.47, s32[384,128]{1,0:T(8,128)S(1)} %bitcast.36, s32[384,128]{1,0:T(8,128)S(1)} %bitcast.41, s32[384,128]{1,0:T(8,128)S(1)} %collective-permute-done.2.refs_0_.refs_3_.refs_1_.refs_4_, ...), custom_call_target="tpu_custom_call" | custom-call | tf_op jit(solution)/shard_map/early/pallas_call | solution.py:295
  102.6 0.0 collective-permute-done.3.refs_0_.refs_3_.refs_1_
  102.6 1.2 late.8
  103.8 20.4 %all_to_all.34 = s32[128,1,384]{2,1,0:T(1,128)S(1)} all-to-all(s32[128,1,384]{2,1,0:T(1,128)S(1)} %bitcast.54), channel_id=1, replica_groups=mesh['area_0'=4,'area_1'=4,'area_2'=2,'rank'=8] {'area_0','area_1','rank'}, dimensions={0} | all-to-all | bytes 393216 | tf_op jit(solution)/shard_map/all_to_all | solution.py:256
  124.2 0.0 copy-start.4
  124.2 0.0 collective-permute-start.4
  124.2 2.0 %early.9.refs_3_ = f32[96,128]{1,0:T(8,128)S(1)} custom-call(s32[1,128]{1,0:T(1,128)S(1)} %get-tuple-element.23.plan_ref, s32[384,128]{1,0:T(8,128)S(1)} %bitcast.50, s32[384,128]{1,0:T(8,128)S(1)} %bitcast.48, s32[384,128]{1,0:T(8,128)S(1)} %bitcast.37, s32[384,128]{1,0:T(8,128)S(1)} %collective-permute-done.3.refs_0_.refs_3_.refs_1_, ...), custom_call_target="tpu_custom_call" | custom-call | tf_op jit(solution)/shard_map/early/pallas_call | solution.py:295
  126.2 0.0 collective-permute-done.4.refs_0_
  126.2 1.8 %late.9 = (f32[48,128]{1,0:T(8,128)S(1)}, f32[256,128]{1,0:T(8,128)S(1)}, f32[16,128]{1,0:T(8,128)}) custom-call(s32[1,128]{1,0:T(1,128)S(1)} %get-tuple-element.21.plan_ref, s32[384,128]{1,0:T(8,128)S(1)} %collective-permute-done.4.refs_0_, s32[384,128]{1,0:T(8,128)S(1)} %collective-permute-done.3.refs_0_.refs_3_.refs_1_, bf16[16384,128]{1,0:T(8,128)(2,1)S(1)} %bitcast.33, ...), custom_call_target="tpu_custom_call" | custom-call | tf_op jit(solution)/shard_map/late/pallas_call | solution.py:302
  128.0 18.7 %all_to_all.35 = f32[256,1,128]{2,1,0:T(1,128)S(1)} all-to-all(f32[256,1,128]{2,1,0:T(1,128)S(1)} %bitcast.57), channel_id=1, replica_groups=mesh['area_0'=4,'area_1'=4,'area_2'=2,'rank'=8] {'area_0','area_1','area..., dimensions={0} | all-to-all | bytes 262144 | tf_op jit(solution)/shard_map/all_to_all | solution.py:256
  146.7 0.0 copy-done.4
  146.7 0.8 rates.1
  (2 shorter events, 0.0 us)
Async XLA Ops:
  1.5 28.4 %copy-start = (bf16[1,128,128,128]{3,2,1,0:T(8,128)(2,1)S(1)}, bf16[1,128,128,128]{3,2,1,0:T(8,128)(2,1)}, u32[]{:S(2)}) copy-start(bf16[1,128,128,128]{3,2,1,0:T(8,128)(2,1)} %param.13) | copy-start | bytes 12582916
  1.7 30.2 %copy-start.1 = (f32[48,128]{1,0:T(8,128)S(1)}, f32[48,128]{1,0:T(8,128)}, u32[]{:S(2)}) copy-start(f32[48,128]{1,0:T(8,128)} %refs_3_.1) | copy-start | bytes 73732
  1.7 30.2 %copy-start.2 = (s32[128]{0:T(128)S(1)}, s32[128]{0:T(128)}, u32[]{:S(2)}) copy-start(s32[128]{0:T(128)} %param.11) | copy-start | bytes 1540
  1.7 30.2 %copy-start.3 = (s32[128]{0:T(128)S(1)}, s32[128]{0:T(128)}, u32[]{:S(2)}) copy-start(s32[128]{0:T(128)} %param.12) | copy-start | bytes 1540
  29.9 2.0 %collective-permute-start = (s32[384,128]{1,0:T(8,128)S(1)}, s32[384,128]{1,0:T(8,128)S(1)}, u32[]{:S(2)}, u32[]{:S(2)}) collective-permute-start(s32[384,128]{1,0:T(8,128)S(1)} %bitcast.42), channel_id=1, source_target_pairs={{0,8},{8,0},{1,9},{9,1},{2,10},{10,2},{3,11},{11,3},{4,12},{12,4},... | collective-permute-start | bytes 589832 | tf_op jit(solution)/shard_map/ppermute | solution.py:292
  53.5 2.0 %collective-permute-start.1 = (s32[384,128]{1,0:T(8,128)S(1)}, s32[384,128]{1,0:T(8,128)S(1)}, u32[]{:S(2)}, u32[]{:S(2)}) collective-permute-start(s32[384,128]{1,0:T(8,128)S(1)} %bitcast.38), channel_id=1, source_target_pairs={{0,8},{8,0},{1,9},{9,1},{2,10},{10,2},{3,11},{11,3},{4,12},{12,4},... | collective-permute-start | bytes 589832 | tf_op jit(solution)/shard_map/ppermute | solution.py:292
  77.0 2.0 %collective-permute-start.2 = (s32[384,128]{1,0:T(8,128)S(1)}, s32[384,128]{1,0:T(8,128)S(1)}, u32[]{:S(2)}, u32[]{:S(2)}) collective-permute-start(s32[384,128]{1,0:T(8,128)S(1)} %bitcast.34), channel_id=1, source_target_pairs={{0,8},{8,0},{1,9},{9,1},{2,10},{10,2},{3,11},{11,3},{4,12},{12,4},... | collective-permute-start | bytes 589832 | tf_op jit(solution)/shard_map/ppermute | solution.py:292
  100.6 2.0 %collective-permute-start.3 = (s32[384,128]{1,0:T(8,128)S(1)}, s32[384,128]{1,0:T(8,128)S(1)}, u32[]{:S(2)}, u32[]{:S(2)}) collective-permute-start(s32[384,128]{1,0:T(8,128)S(1)} %bitcast.46), channel_id=1, source_target_pairs={{0,8},{8,0},{1,9},{9,1},{2,10},{10,2},{3,11},{11,3},{4,12},{12,4},... | collective-permute-start | bytes 589832 | tf_op jit(solution)/shard_map/ppermute | solution.py:292
  124.2 22.5 %copy-start.4 = (s32[256,1]{0,1:T(1,128)S(1)}, s32[256,1]{0,1:T(1,128)}, u32[]{:S(2)}) copy-start(s32[256,1]{0,1:T(1,128)} %param.17) | copy-start | bytes 3076
  124.2 2.0 %collective-permute-start.4 = (s32[384,128]{1,0:T(8,128)S(1)}, s32[384,128]{1,0:T(8,128)S(1)}, u32[]{:S(2)}, u32[]{:S(2)}) collective-permute-start(s32[384,128]{1,0:T(8,128)S(1)} %bitcast.49), channel_id=1, source_target_pairs={{0,8},{8,0},{1,9},{9,1},{2,10},{10,2},{3,11},{11,3},{4,12},{12,4},... | collective-permute-start | bytes 589832 | tf_op jit(solution)/shard_map/ppermute | solution.py:292

commit v4 on v3

--- a/solution.py
+++ b/solution.py
@@ -14,7 +14,8 @@
 TRIALS = 48
 SLOTS = 128
 THRESHOLD = 200.0
-GROUP = 16
+GROUP = 48
+PLAN = 144
 WORDS = 3
 HALF = 128 * WORDS
 TABLE = 2 * HALF
@@ -22,7 +23,6 @@
 PLANE = ("area_0", "area_1", "rank")
 
 VMEM = pl.BlockSpec(memory_space=pltpu.VMEM)
-SMEM = pl.BlockSpec(memory_space=pltpu.SMEM)
 
 
 def kernel_call(body, outs, ins, scratch, name, limit, cost=None):
@@ -99,24 +99,20 @@
 
 
 def plan(slots, out_refs):
-    kind = jnp.right_shift(slots, 20)
+    kind = jnp.broadcast_to(jnp.right_shift(slots, 20), (SLOTS, SLOTS))
     code = jnp.bitwise_and(slots, (1 << 20) - 1)
-
-    def column(row):
-        return jnp.transpose(jnp.broadcast_to(row, (SLOTS, SLOTS)))
-
     sub, lane = row_ids(SLOTS), lane_ids(SLOTS)
-    kind_col, code_col = column(kind), column(code)
-    kind_row = jnp.broadcast_to(kind, (SLOTS, SLOTS))
-    before = jnp.where((kind_row == kind_col) & (lane < sub), 1, 0)
-    rank_col = jnp.sum(before, axis=1, keepdims=True, dtype=jnp.int32)
+    before = jnp.where((jnp.transpose(kind) == kind) & (sub < lane), 1, 0)
+    rank = jnp.sum(before, axis=0, keepdims=True, dtype=jnp.int32)
     nothing = NDELAY * TABLE * SLOTS
-    for k in range(2):
-        hit = (kind_col == k) & (rank_col == lane)
-        codes = jnp.sum(jnp.where(hit, code_col - nothing, 0), axis=0, keepdims=True, dtype=jnp.int32)
-        count = jnp.sum(jnp.where(kind == k, 1, 0), axis=1, keepdims=True, dtype=jnp.int32)
-        codes = codes + nothing + jnp.where(lane_ids(1) == 0, jnp.left_shift(count, 20), 0)
-        out_refs[k][...] = codes
+    for k, out_ref in enumerate(out_refs):
+        hit = (kind == k) & (rank == sub)
+        codes = jnp.sum(jnp.where(hit, code - nothing, 0), axis=1, keepdims=True, dtype=jnp.int32)
+        count = jnp.where(kind == k, 1, 0)
+        count = jnp.sum(count, axis=1, keepdims=True, dtype=jnp.int32)
+        codes = codes + nothing + jnp.where(sub == 0, jnp.left_shift(count, 20), 0)
+        out_ref[pl.ds(0, SLOTS), :] = codes
+        out_ref[pl.ds(SLOTS, PLAN - SLOTS), :] = jnp.full((PLAN - SLOTS, SLOTS), nothing, jnp.int32)
 
 
 def shifted(older, newer):
@@ -141,7 +137,7 @@
     def group(i, acc):
         left, right = [], []
         for k in range(GROUP):
-            code = plan_ref[0, i * GROUP + k]
+            code = plan_ref[i * GROUP + k, 0]
             base = jnp.bitwise_and(jnp.right_shift(code, 7), (1 << 13) - 1)
             slot = jnp.bitwise_and(code, SLOTS - 1)
             rows = []
@@ -156,7 +152,8 @@
         return acc + jnp.dot(left, right, preferred_element_type=jnp.float32)
 
     zero = jnp.zeros((DMIN * TRIALS, BLOCK), jnp.float32)
-    groups = jnp.right_shift(jnp.right_shift(plan_ref[0, 0], 20) + (GROUP - 1), 4)
+    count = jnp.right_shift(plan_ref[0, 0], 20)
+    groups = sum((count > i).astype(jnp.int32) for i in range(0, SLOTS, GROUP))
     return lax.fori_loop(0, groups, group, zero)
 
 
@@ -184,7 +181,8 @@
         rest = refs[min(n_hist, 2) :]
         w_ref, early_ref, v_ref, drive_ref, leak_ref = rest[:5]
         count_ref = rest[5] if number else None
-        v_out, pk_out, count_out, table = rest[-4:]
+        v_out, pk_out = rest[-3 - (not last) : -1 - (not last)]
+        table = rest[-1]
 
         for lag in range(2):
             fill(table, lag, 1, newer, older)
@@ -220,8 +218,9 @@
         for step in range(DMIN):
             total = jnp.sum(spikes[step].astype(jnp.float32), axis=0, keepdims=True)
             counts = jnp.where(row == number * DMIN + step, total, counts)
-        count_out[...] = counts
-        if last:
+        if not last:
+            rest[-2][...] = counts
+        else:
             total = jnp.sum(counts, axis=1, keepdims=True)
             total = jnp.where(row == lane_ids(16), total, 0.0)
             total = jnp.sum(total, axis=0, keepdims=True)
@@ -265,7 +264,7 @@
     sums = jax.ShapeDtypeStruct((DMIN * TRIALS, BLOCK), jnp.float32)
     blocks = area_of_block.shape[0]
     table = pltpu.VMEM((NDELAY * TABLE + 8, BLOCK), jnp.int32)
-    codes = jax.ShapeDtypeStruct((1, SLOTS), jnp.int32)
+    codes = jax.ShapeDtypeStruct((PLAN, SLOTS), jnp.int32)
 
     flat = weights.reshape(SLOTS * BLOCK, BLOCK)
     drive = drive.reshape(1, BLOCK)
@@ -293,21 +292,20 @@
         own = [mine] + own[:2]
         n_hist = len(own)
         early = kernel_call(
-            early_body(n_hist), sums, [SMEM] + [VMEM] * (2 * n_hist), [table], "early", 24
+            early_body(n_hist), sums, [VMEM] + [VMEM] * (2 * n_hist), [table], "early", 24
         )(early_plan, *own, *other[: n_hist - 1], flat)
         other = [theirs] + other[:2]
         last = number == STEPS // DMIN - 1
         out = jax.ShapeDtypeStruct((blocks, BLOCK), jnp.float32) if last else words
         rest = [*other[:2], flat, early, v, drive, leak_shift, *counts]
-        v, copies, count = kernel_call(
+        v, copies, *counts = kernel_call(
             late_body(number, n_hist),
-            (volts, out, totals),
-            [SMEM] + [VMEM] * len(rest),
+            (volts, out) if last else (volts, out, totals),
+            [VMEM] + [VMEM] * len(rest),
             [table],
             "late",
             24,
         )(late_plan, *rest)
-        counts = [count]
     everyone = exchanged(copies, AREA_RANK)
     rates = jax.ShapeDtypeStruct((STEPS, AREAS), jnp.float32)
     rates, v = kernel_call(rates_body, (rates, volts), [VMEM] * 3, [], "rates", 8)(

time: 149 us -> 142 us (0.953)
  Pallas kernels: 17.4 us -> 10.6 us
    pallas_call x10, Pallas kernels: 16.3 us -> 9.46 us  [the longest x5 6.07 us: on_device(): kernel_call(early_body(n_hist), sums, [VMEM] + [VMEM] * (2 * n_hist), [ta...]
  transfers between devices with their start and end apart: 5 -> 5, of which waited for: 0 -> 5; matrix products, arithmetic and copies ran while one was open for 0% -> 0% of each run, Pallas kernels for 7% -> 4%
where the time goes in v4:
time: 142 us; the launch traced here: 140 us
  blocking collectives  127 us (89%)
  Pallas kernels  10.6 us (7%)
    all_to_all x6, blocking collectives, exchanged(): lax.all_to_all(pieces, axes, split_axis=0, concat_axis=0)  127 us
    pallas_call x5, Pallas kernels, on_device(): kernel_call(early_body(n_hist), sums, [VMEM] + [VMEM] * (2 * n_hist), [ta...  6.07 us
    pallas_call x5, Pallas kernels, on_device(): kernel_call(late_body(number, n_hist), (volts, out) if last else (volts,...  3.38 us
  transfers between devices with their start and end apart: 5, of which 5 were waited for; matrix products, arithmetic and copies ran while one was open for 0% of the time, Pallas kernels for 4%

profile of v4, /device:TPU:32, one launch (start us, length us, event | category | flops | bytes accessed | tf_op | source)
XLA Modules:
  0.0 140.4 jit_solution(8923008750647506044)
XLA Ops:
  0.7 0.8 select_select_fusion.input_ref
  1.5 0.0 copy-start
  1.5 0.3 first.1
  1.8 0.0 copy-start.1
  1.8 0.0 copy-start.2
  1.8 0.0 copy-start.3
  1.8 28.2 %all_to_all.30 = s32[128,1,384]{2,1,0:T(1,128)S(1)} all-to-all(s32[128,1,384]{2,1,0:T(1,128)S(1)} %bitcast.55), channel_id=1, replica_groups=mesh['area_0'=4,'area_1'=4,'area_2'=2,'rank'=8] {'area_0','area_1','rank'}, dimensions={0} | all-to-all | bytes 393216 | tf_op jit(solution)/shard_map/all_to_all | solution.py:255
  30.0 0.0 collective-permute-start
  30.0 0.0 copy-done
  30.0 1.2 early.5.refs_2_
  31.2 0.2 collective-permute-done.refs_0_.refs_2_.refs_1_.refs_4_
  31.4 0.0 copy-done.1
  31.4 0.0 copy-done.2
  31.5 0.0 copy-done.3
  31.5 0.7 late.5
  32.1 19.9 %all_to_all.31 = s32[128,1,384]{2,1,0:T(1,128)S(1)} all-to-all(s32[128,1,384]{2,1,0:T(1,128)S(1)} %bitcast.56), channel_id=1, replica_groups=mesh['area_0'=4,'area_1'=4,'area_2'=2,'rank'=8] {'area_0','area_1','rank'}, dimensions={0} | all-to-all | bytes 393216 | tf_op jit(solution)/shard_map/all_to_all | solution.py:255
  52.0 0.0 collective-permute-start.1
  52.0 1.2 early.6.refs_3_
  53.2 0.2 collective-permute-done.1.refs_0_.refs_3_.refs_1_.refs_4_
  53.5 0.7 late.6
  54.2 19.9 %all_to_all.32 = s32[128,1,384]{2,1,0:T(1,128)S(1)} all-to-all(s32[128,1,384]{2,1,0:T(1,128)S(1)} %bitcast.52), channel_id=1, replica_groups=mesh['area_0'=4,'area_1'=4,'area_2'=2,'rank'=8] {'area_0','area_1','rank'}, dimensions={0} | all-to-all | bytes 393216 | tf_op jit(solution)/shard_map/all_to_all | solution.py:255
  74.1 0.0 collective-permute-start.2
  74.1 1.2 early.7.refs_3_
  75.3 0.2 collective-permute-done.2.refs_0_.refs_3_.refs_1_.refs_4_
  75.5 0.7 late.7
  76.2 20.1 %all_to_all.33 = s32[128,1,384]{2,1,0:T(1,128)S(1)} all-to-all(s32[128,1,384]{2,1,0:T(1,128)S(1)} %bitcast.53), channel_id=1, replica_groups=mesh['area_0'=4,'area_1'=4,'area_2'=2,'rank'=8] {'area_0','area_1','rank'}, dimensions={0} | all-to-all | bytes 393216 | tf_op jit(solution)/shard_map/all_to_all | solution.py:255
  96.3 0.0 collective-permute-start.3
  96.3 1.2 early.8.refs_3_
  97.5 0.2 collective-permute-done.3.refs_0_.refs_3_.refs_1_
  97.7 0.7 late.8
  98.4 19.9 %all_to_all.34 = s32[128,1,384]{2,1,0:T(1,128)S(1)} all-to-all(s32[128,1,384]{2,1,0:T(1,128)S(1)} %bitcast.54), channel_id=1, replica_groups=mesh['area_0'=4,'area_1'=4,'area_2'=2,'rank'=8] {'area_0','area_1','rank'}, dimensions={0} | all-to-all | bytes 393216 | tf_op jit(solution)/shard_map/all_to_all | solution.py:255
  118.4 0.0 copy-start.4
  118.4 0.0 collective-permute-start.4
  118.4 1.2 early.9.refs_3_
  119.6 0.2 collective-permute-done.4.refs_0_
  119.8 0.7 late.9
  120.5 19.0 %all_to_all.35 = f32[256,1,128]{2,1,0:T(1,128)S(1)} all-to-all(f32[256,1,128]{2,1,0:T(1,128)S(1)} %bitcast.57), channel_id=1, replica_groups=mesh['area_0'=4,'area_1'=4,'area_2'=2,'rank'=8] {'area_0','area_1','area..., dimensions={0} | all-to-all | bytes 262144 | tf_op jit(solution)/shard_map/all_to_all | solution.py:255
  139.6 0.0 copy-done.4
  139.6 0.8 rates.1
  (2 shorter events, 0.0 us)
Async XLA Ops:
  1.5 28.6 %copy-start = (bf16[1,128,128,128]{3,2,1,0:T(8,128)(2,1)S(1)}, bf16[1,128,128,128]{3,2,1,0:T(8,128)(2,1)}, u32[]{:S(2)}) copy-start(bf16[1,128,128,128]{3,2,1,0:T(8,128)(2,1)} %param.13) | copy-start | bytes 12582916
  1.8 29.6 %copy-start.1 = (f32[48,128]{1,0:T(8,128)S(1)}, f32[48,128]{1,0:T(8,128)}, u32[]{:S(2)}) copy-start(f32[48,128]{1,0:T(8,128)} %refs_3_.1) | copy-start | bytes 73732
  1.8 29.6 %copy-start.2 = (s32[128]{0:T(128)S(1)}, s32[128]{0:T(128)}, u32[]{:S(2)}) copy-start(s32[128]{0:T(128)} %param.11) | copy-start | bytes 1540
  1.8 29.6 %copy-start.3 = (s32[128]{0:T(128)S(1)}, s32[128]{0:T(128)}, u32[]{:S(2)}) copy-start(s32[128]{0:T(128)} %param.12) | copy-start | bytes 1540
  30.0 1.4 %collective-permute-start = (s32[384,128]{1,0:T(8,128)S(1)}, s32[384,128]{1,0:T(8,128)S(1)}, u32[]{:S(2)}, u32[]{:S(2)}) collective-permute-start(s32[384,128]{1,0:T(8,128)S(1)} %bitcast.34), channel_id=1, source_target_pairs={{0,8},{8,0},{1,9},{9,1},{2,10},{10,2},{3,11},{11,3},{4,12},{12,4},... | collective-permute-start | bytes 589832 | tf_op jit(solution)/shard_map/ppermute | solution.py:291
  52.0 1.4 %collective-permute-start.1 = (s32[384,128]{1,0:T(8,128)S(1)}, s32[384,128]{1,0:T(8,128)S(1)}, u32[]{:S(2)}, u32[]{:S(2)}) collective-permute-start(s32[384,128]{1,0:T(8,128)S(1)} %bitcast.38), channel_id=1, source_target_pairs={{0,8},{8,0},{1,9},{9,1},{2,10},{10,2},{3,11},{11,3},{4,12},{12,4},... | collective-permute-start | bytes 589832 | tf_op jit(solution)/shard_map/ppermute | solution.py:291
  74.1 1.4 %collective-permute-start.2 = (s32[384,128]{1,0:T(8,128)S(1)}, s32[384,128]{1,0:T(8,128)S(1)}, u32[]{:S(2)}, u32[]{:S(2)}) collective-permute-start(s32[384,128]{1,0:T(8,128)S(1)} %bitcast.42), channel_id=1, source_target_pairs={{0,8},{8,0},{1,9},{9,1},{2,10},{10,2},{3,11},{11,3},{4,12},{12,4},... | collective-permute-start | bytes 589832 | tf_op jit(solution)/shard_map/ppermute | solution.py:291
  96.3 1.4 %collective-permute-start.3 = (s32[384,128]{1,0:T(8,128)S(1)}, s32[384,128]{1,0:T(8,128)S(1)}, u32[]{:S(2)}, u32[]{:S(2)}) collective-permute-start(s32[384,128]{1,0:T(8,128)S(1)} %bitcast.46), channel_id=1, source_target_pairs={{0,8},{8,0},{1,9},{9,1},{2,10},{10,2},{3,11},{11,3},{4,12},{12,4},... | collective-permute-start | bytes 589832 | tf_op jit(solution)/shard_map/ppermute | solution.py:291
  118.4 21.2 %copy-start.4 = (s32[256,1]{0,1:T(1,128)S(1)}, s32[256,1]{0,1:T(1,128)}, u32[]{:S(2)}) copy-start(s32[256,1]{0,1:T(1,128)} %param.17) | copy-start | bytes 3076
  118.4 1.4 %collective-permute-start.4 = (s32[384,128]{1,0:T(8,128)S(1)}, s32[384,128]{1,0:T(8,128)S(1)}, u32[]{:S(2)}, u32[]{:S(2)}) collective-permute-start(s32[384,128]{1,0:T(8,128)S(1)} %bitcast.49), channel_id=1, source_target_pairs={{0,8},{8,0},{1,9},{9,1},{2,10},{10,2},{3,11},{11,3},{4,12},{12,4},... | collective-permute-start | bytes 589832 | tf_op jit(solution)/shard_map/ppermute | solution.py:291

commit v5 on v4

--- a/solution.py
+++ b/solution.py
@@ -19,8 +19,8 @@
 WORDS = 3
 HALF = 128 * WORDS
 TABLE = 2 * HALF
-AREA_RANK = ("area_0", "area_1", "area_2", "rank")
-PLANE = ("area_0", "area_1", "rank")
+CHIPS = (4, 4, 8)
+CORE = 8
 
 VMEM = pl.BlockSpec(memory_space=pltpu.VMEM)
 
@@ -85,13 +85,18 @@
         packed = packed | jnp.left_shift(half.astype(jnp.int32), 16 * step)
     store_copies(out_ref, [packed[j : j + 1] for j in range(WORDS)])
     rows = [input_ref[8 + i : 9 + i, :] for i in range(4)]
-    plan(slot_codes(lax.axis_size("rank"), *rows), (early_ref, late_ref))
-
-
-def slot_codes(ranks, pre, mask, delay, core):
+    plan(slot_codes(*rows), (early_ref, late_ref))
+
+
+def chip_order(block):
+    y, x, z = block // 64, block // 16 % 4, block % 8
+    return (x * CHIPS[2] + z) * CHIPS[0] + y
+
+
+def slot_codes(pre, mask, delay, device):
     lag = delay - DMIN
-    other = jnp.bitwise_xor(pre // ranks % 2, core)
-    place = pre // (2 * ranks) * ranks + pre % ranks
+    other = jnp.bitwise_and(jnp.bitwise_xor(pre, device), CORE) // CORE
+    place = chip_order(pre)
     base = lag * TABLE + other * HALF + place * WORDS
     late = jnp.where((other == 1) & (lag < 2), 1, 0)
     kind = jnp.where(mask == 1, late, 2)
@@ -248,11 +253,14 @@
     out_ref[...] = jnp.transpose(rates)[:STEPS, :AREAS]
 
 
-def exchanged(copies, axes):
+def exchanged(copies, groups):
     rows = copies.shape[0]
-    peers = lax.axis_size(axes)
+    peers = len(groups[0])
     pieces = copies.reshape(peers, 1, rows // peers * BLOCK)
-    return lax.all_to_all(pieces, axes, split_axis=0, concat_axis=0).reshape(rows, BLOCK)
+    got = lax.all_to_all(
+        pieces, "device", split_axis=0, concat_axis=0, axis_index_groups=groups
+    )
+    return got.reshape(rows, BLOCK)
 
 
 def on_device(
@@ -273,8 +281,8 @@
     counts = []
     bits = jnp.transpose(initial_bits, (0, 2, 1)).reshape(8, TRIALS)
     first_input = jnp.pad(bits, ((0, 8), (0, BLOCK - TRIALS)))
-    core = lax.broadcast(lax.axis_index("area_2"), (1, BLOCK))
-    for row, values in enumerate((pre_block, block_mask, delay, core), 8):
+    device = lax.broadcast(lax.axis_index("device"), (1, BLOCK))
+    for row, values in enumerate((pre_block, block_mask, delay, device), 8):
         first_input = jnp.where(row_ids(16) == row, values, first_input)
     copies, early_plan, late_plan = kernel_call(
         first_body,
@@ -286,9 +294,11 @@
         pl.CostEstimate(flops=10**10, bytes_accessed=1 << 18, transcendentals=0),
     )(first_input)
     own, other = [], []
+    devices = range(lax.axis_size("device"))
+    chips = [sorted((d for d in devices if d // CORE % 2 == c), key=chip_order) for c in range(2)]
     for number in range(STEPS // DMIN):
-        mine = exchanged(copies, PLANE)
-        theirs = lax.ppermute(mine, "area_2", [(0, 1), (1, 0)])
+        mine = exchanged(copies, chips)
+        theirs = lax.ppermute(mine, "device", [(d, d ^ CORE) for d in devices])
         own = [mine] + own[:2]
         n_hist = len(own)
         early = kernel_call(
@@ -306,7 +316,7 @@
             "late",
             24,
         )(late_plan, *rest)
-    everyone = exchanged(copies, AREA_RANK)
+    everyone = exchanged(copies, [list(devices)])
     rates = jax.ShapeDtypeStruct((STEPS, AREAS), jnp.float32)
     rates, v = kernel_call(rates_body, (rates, volts), [VMEM] * 3, [], "rates", 8)(
         everyone, area_of_block.reshape(1, blocks), v
@@ -315,23 +325,22 @@
 
 
 def solution(mesh):
-    split = Mesh(
-        mesh.devices.reshape(4, 4, 2, mesh.shape["rank"]), ("area_0", "area_1", "area_2", "rank")
-    )
+    split = P("device")
+    columns = P(None, "device")
     return jax.shard_map(
         on_device,
-        mesh=split,
+        mesh=Mesh(mesh.devices.reshape(-1), ("device",)),
         in_specs=(
-            P(None, None, AREA_RANK),
-            P(None, AREA_RANK),
-            P(AREA_RANK),
-            P(AREA_RANK),
-            P(AREA_RANK, None, None, None),
-            P(AREA_RANK, None),
-            P(AREA_RANK, None),
-            P(AREA_RANK, None),
+            P(None, None, "device"),
+            columns,
+            split,
+            split,
+            split,
+            split,
+            split,
+            split,
             P(),
         ),
-        out_specs=(P(None, AREA_RANK), P()),
+        out_specs=(columns, P()),
         check_vma=False,
     )

time: 142 us -> 141 us (level)
  no operation moved by 1% of the time
where the time goes in v5:
time: 141 us; the launch traced here: 139 us
  blocking collectives  126 us (89%)
  Pallas kernels  10.6 us (8%)
    all_to_all x6, blocking collectives, exchanged(): lax.all_to_all(pieces, 'device', split_axis=0, concat_axis=0, axis_index_...  126 us
    pallas_call x5, Pallas kernels, on_device(): kernel_call(early_body(n_hist), sums, [VMEM] + [VMEM] * (2 * n_hist), [ta...  6.09 us
    pallas_call x5, Pallas kernels, on_device(): kernel_call(late_body(number, n_hist), (volts, out) if last else (volts,...  3.39 us
  transfers between devices with their start and end apart: 5, of which 5 were waited for; matrix products, arithmetic and copies ran while one was open for 0% of the time, Pallas kernels for 4%

profile of v5, /device:TPU:32, one launch (start us, length us, event | category | flops | bytes accessed | tf_op | source)
XLA Modules:
  0.0 139.1 jit_solution(13547510780889919628)
XLA Ops:
  0.7 0.8 select_select_fusion.input_ref
  1.5 0.0 copy-start
  1.5 0.3 first.1
  1.8 0.0 copy-start.1
  1.8 0.0 copy-start.2
  1.8 0.0 copy-start.3
  1.8 28.0 %all_to_all.30 = s32[128,1,384]{2,1,0:T(1,128)S(1)} all-to-all(s32[128,1,384]{2,1,0:T(1,128)S(1)} %bitcast.55), channel_id=1, replica_groups={{0,64,128,192,1,65,129,193,2,66,130,194,3,67,131,195,4,68,132,196,5,69,..., dimensions={0} | all-to-all | bytes 393216 | tf_op jit(solution)/shard_map/all_to_all | solution.py:260
  29.9 0.0 collective-permute-start
  29.9 0.0 copy-done
  29.9 1.2 early.5.refs_2_
  31.1 0.2 collective-permute-done.refs_0_.refs_2_.refs_1_.refs_4_
  31.3 0.0 copy-done.1
  31.3 0.0 copy-done.2
  31.3 0.0 copy-done.3
  31.3 0.7 late.5
  32.0 19.7 %all_to_all.31 = s32[128,1,384]{2,1,0:T(1,128)S(1)} all-to-all(s32[128,1,384]{2,1,0:T(1,128)S(1)} %bitcast.56), channel_id=1, replica_groups={{0,64,128,192,1,65,129,193,2,66,130,194,3,67,131,195,4,68,132,196,5,69,..., dimensions={0} | all-to-all | bytes 393216 | tf_op jit(solution)/shard_map/all_to_all | solution.py:260
  51.7 0.0 collective-permute-start.1
  51.7 1.2 early.6.refs_3_
  52.9 0.2 collective-permute-done.1.refs_0_.refs_3_.refs_1_.refs_4_
  53.1 0.7 late.6
  53.8 19.7 %all_to_all.32 = s32[128,1,384]{2,1,0:T(1,128)S(1)} all-to-all(s32[128,1,384]{2,1,0:T(1,128)S(1)} %bitcast.52), channel_id=1, replica_groups={{0,64,128,192,1,65,129,193,2,66,130,194,3,67,131,195,4,68,132,196,5,69,..., dimensions={0} | all-to-all | bytes 393216 | tf_op jit(solution)/shard_map/all_to_all | solution.py:260
  73.5 0.0 collective-permute-start.2
  73.5 1.2 early.7.refs_3_
  74.7 0.2 collective-permute-done.2.refs_0_.refs_3_.refs_1_.refs_4_
  74.9 0.7 late.7
  75.6 19.9 %all_to_all.33 = s32[128,1,384]{2,1,0:T(1,128)S(1)} all-to-all(s32[128,1,384]{2,1,0:T(1,128)S(1)} %bitcast.53), channel_id=1, replica_groups={{0,64,128,192,1,65,129,193,2,66,130,194,3,67,131,195,4,68,132,196,5,69,..., dimensions={0} | all-to-all | bytes 393216 | tf_op jit(solution)/shard_map/all_to_all | solution.py:260
  95.4 0.0 collective-permute-start.3
  95.4 1.2 early.8.refs_3_
  96.7 0.2 collective-permute-done.3.refs_0_.refs_3_.refs_1_
  96.9 0.7 late.8
  97.5 19.7 %all_to_all.34 = s32[128,1,384]{2,1,0:T(1,128)S(1)} all-to-all(s32[128,1,384]{2,1,0:T(1,128)S(1)} %bitcast.54), channel_id=1, replica_groups={{0,64,128,192,1,65,129,193,2,66,130,194,3,67,131,195,4,68,132,196,5,69,..., dimensions={0} | all-to-all | bytes 393216 | tf_op jit(solution)/shard_map/all_to_all | solution.py:260
  117.2 0.0 copy-start.4
  117.2 0.0 collective-permute-start.4
  117.2 1.2 early.9.refs_3_
  118.5 0.2 collective-permute-done.4.refs_0_
  118.7 0.7 late.9
  119.4 18.8 %all_to_all.35 = f32[256,1,128]{2,1,0:T(1,128)S(1)} all-to-all(f32[256,1,128]{2,1,0:T(1,128)S(1)} %bitcast.57), channel_id=1, replica_groups={{0,1,2,3,4,5,6,7,8,9,10,11,12,13,14,15,16,17,18,19,20,21,22,23,24,25,26..., dimensions={0} | all-to-all | bytes 262144 | tf_op jit(solution)/shard_map/all_to_all | solution.py:260
  138.2 0.0 copy-done.4
  138.2 0.8 rates.1
  (2 shorter events, 0.0 us)
Async XLA Ops:
  1.5 28.4 %copy-start = (bf16[1,128,128,128]{3,2,1,0:T(8,128)(2,1)S(1)}, bf16[1,128,128,128]{3,2,1,0:T(8,128)(2,1)}, u32[]{:S(2)}) copy-start(bf16[1,128,128,128]{3,2,1,0:T(8,128)(2,1)} %param.13) | copy-start | bytes 12582916
  1.8 29.5 %copy-start.1 = (f32[48,128]{1,0:T(8,128)S(1)}, f32[48,128]{1,0:T(8,128)}, u32[]{:S(2)}) copy-start(f32[48,128]{1,0:T(8,128)} %refs_3_.1) | copy-start | bytes 73732
  1.8 29.5 %copy-start.2 = (s32[128]{0:T(128)S(1)}, s32[128]{0:T(128)}, u32[]{:S(2)}) copy-start(s32[128]{0:T(128)} %param.11) | copy-start | bytes 1540
  1.8 29.5 %copy-start.3 = (s32[128]{0:T(128)S(1)}, s32[128]{0:T(128)}, u32[]{:S(2)}) copy-start(s32[128]{0:T(128)} %param.12) | copy-start | bytes 1540
  29.9 1.4 %collective-permute-start = (s32[384,128]{1,0:T(8,128)S(1)}, s32[384,128]{1,0:T(8,128)S(1)}, u32[]{:S(2)}, u32[]{:S(2)}) collective-permute-start(s32[384,128]{1,0:T(8,128)S(1)} %bitcast.34), channel_id=1, source_target_pairs={{0,8},{1,9},{2,10},{3,11},{4,12},{5,13},{6,14},{7,15},{8,0},{9,1},... | collective-permute-start | bytes 589832 | tf_op jit(solution)/shard_map/ppermute | solution.py:301
  51.7 1.4 %collective-permute-start.1 = (s32[384,128]{1,0:T(8,128)S(1)}, s32[384,128]{1,0:T(8,128)S(1)}, u32[]{:S(2)}, u32[]{:S(2)}) collective-permute-start(s32[384,128]{1,0:T(8,128)S(1)} %bitcast.38), channel_id=1, source_target_pairs={{0,8},{1,9},{2,10},{3,11},{4,12},{5,13},{6,14},{7,15},{8,0},{9,1},... | collective-permute-start | bytes 589832 | tf_op jit(solution)/shard_map/ppermute | solution.py:301
  73.5 1.4 %collective-permute-start.2 = (s32[384,128]{1,0:T(8,128)S(1)}, s32[384,128]{1,0:T(8,128)S(1)}, u32[]{:S(2)}, u32[]{:S(2)}) collective-permute-start(s32[384,128]{1,0:T(8,128)S(1)} %bitcast.42), channel_id=1, source_target_pairs={{0,8},{1,9},{2,10},{3,11},{4,12},{5,13},{6,14},{7,15},{8,0},{9,1},... | collective-permute-start | bytes 589832 | tf_op jit(solution)/shard_map/ppermute | solution.py:301
  95.4 1.4 %collective-permute-start.3 = (s32[384,128]{1,0:T(8,128)S(1)}, s32[384,128]{1,0:T(8,128)S(1)}, u32[]{:S(2)}, u32[]{:S(2)}) collective-permute-start(s32[384,128]{1,0:T(8,128)S(1)} %bitcast.46), channel_id=1, source_target_pairs={{0,8},{1,9},{2,10},{3,11},{4,12},{5,13},{6,14},{7,15},{8,0},{9,1},... | collective-permute-start | bytes 589832 | tf_op jit(solution)/shard_map/ppermute | solution.py:301
  117.2 21.0 %copy-start.4 = (s32[256,1]{0,1:T(1,128)S(1)}, s32[256,1]{0,1:T(1,128)}, u32[]{:S(2)}) copy-start(s32[256,1]{0,1:T(1,128)} %param.17) | copy-start | bytes 3076
  117.2 1.4 %collective-permute-start.4 = (s32[384,128]{1,0:T(8,128)S(1)}, s32[384,128]{1,0:T(8,128)S(1)}, u32[]{:S(2)}, u32[]{:S(2)}) collective-permute-start(s32[384,128]{1,0:T(8,128)S(1)} %bitcast.49), channel_id=1, source_target_pairs={{0,8},{1,9},{2,10},{3,11},{4,12},{5,13},{6,14},{7,15},{8,0},{9,1},... | collective-permute-start | bytes 589832 | tf_op jit(solution)/shard_map/ppermute | solution.py:301

commit v6 on v5

--- a/solution.py
+++ b/solution.py
@@ -14,15 +14,15 @@
 TRIALS = 48
 SLOTS = 128
 THRESHOLD = 200.0
-GROUP = 48
-PLAN = 144
+EARLY, LATE = 48, 40
+PLAN = 160
 WORDS = 3
 HALF = 128 * WORDS
 TABLE = 2 * HALF
-CHIPS = (4, 4, 8)
 CORE = 8
 
 VMEM = pl.BlockSpec(memory_space=pltpu.VMEM)
+ANY = pl.BlockSpec(memory_space=pl.ANY)
 
 
 def kernel_call(body, outs, ins, scratch, name, limit, cost=None):
@@ -66,7 +66,7 @@
         out_ref[pl.ds(24 * copy, 24), :] = rows
 
 
-def first_body(input_ref, out_ref, early_ref, late_ref):
+def first_body(input_ref, out_ref):
     trial = lane_ids(8, TRIALS)
     which = row_ids(8, TRIALS)
     place = jnp.left_shift(1, trial % 16).astype(jnp.float32)
@@ -84,26 +84,28 @@
         )
         packed = packed | jnp.left_shift(half.astype(jnp.int32), 16 * step)
     store_copies(out_ref, [packed[j : j + 1] for j in range(WORDS)])
-    rows = [input_ref[8 + i : 9 + i, :] for i in range(4)]
-    plan(slot_codes(*rows), (early_ref, late_ref))
-
-
-def chip_order(block):
-    y, x, z = block // 64, block // 16 % 4, block % 8
-    return (x * CHIPS[2] + z) * CHIPS[0] + y
+
+
+def team(block):
+    return (block // 64 + block // 16 + block + block // CORE) % 2
+
+
+def place(block):
+    z = (block + 7 + team(block)) % 8
+    return (block // 16 % 4 * 8 + z) * 4 + block // 64
 
 
 def slot_codes(pre, mask, delay, device):
     lag = delay - DMIN
-    other = jnp.bitwise_and(jnp.bitwise_xor(pre, device), CORE) // CORE
-    place = chip_order(pre)
-    base = lag * TABLE + other * HALF + place * WORDS
+    other = jnp.bitwise_xor(team(pre), team(device))
+    base = lag * TABLE + other * HALF + place(pre) * WORDS
     late = jnp.where((other == 1) & (lag < 2), 1, 0)
     kind = jnp.where(mask == 1, late, 2)
     return kind * (1 << 20) + base * SLOTS + lane_ids(1)
 
 
-def plan(slots, out_refs):
+def plan_body(input_ref, after_ref, *out_refs):
+    slots = slot_codes(*[input_ref[8 + i : 9 + i, :] for i in range(4)])
     kind = jnp.broadcast_to(jnp.right_shift(slots, 20), (SLOTS, SLOTS))
     code = jnp.bitwise_and(slots, (1 << 20) - 1)
     sub, lane = row_ids(SLOTS), lane_ids(SLOTS)
@@ -135,14 +137,14 @@
         table[at, :] = newer[...]
 
 
-def arrivals(plan_ref, table, w_ref):
+def arrivals(plan_ref, size, table, w_ref):
     table[pl.ds(NDELAY * TABLE, 8), :] = jnp.zeros((8, BLOCK), jnp.int32)
     mask = jnp.left_shift(1, row_ids(32))
 
     def group(i, acc):
         left, right = [], []
-        for k in range(GROUP):
-            code = plan_ref[i * GROUP + k, 0]
+        for k in range(size):
+            code = plan_ref[i * size + k, 0]
             base = jnp.bitwise_and(jnp.right_shift(code, 7), (1 << 13) - 1)
             slot = jnp.bitwise_and(code, SLOTS - 1)
             rows = []
@@ -158,7 +160,7 @@
 
     zero = jnp.zeros((DMIN * TRIALS, BLOCK), jnp.float32)
     count = jnp.right_shift(plan_ref[0, 0], 20)
-    groups = sum((count > i).astype(jnp.int32) for i in range(0, SLOTS, GROUP))
+    groups = sum((count > i).astype(jnp.int32) for i in range(0, SLOTS, size))
     return lax.fori_loop(0, groups, group, zero)
 
 
@@ -172,7 +174,7 @@
             fill(table, lag, 0, own[a], own[a + 1] if a < 2 else None)
             if lag >= 2:
                 fill(table, lag, 1, other[a - 1], other[a] if a < 2 else None)
-        out_ref[...] = arrivals(plan_ref, table, w_ref)
+        out_ref[...] = arrivals(plan_ref, EARLY, table, w_ref)
 
     return body
 
@@ -191,7 +193,7 @@
 
         for lag in range(2):
             fill(table, lag, 1, newer, older)
-        current = early_ref[...] + arrivals(plan_ref, table, w_ref)
+        current = early_ref[...] + arrivals(plan_ref, LATE, table, w_ref)
         bit = row_ids(32)
         power = jnp.left_shift(1, jnp.maximum(30 - bit, 0)).astype(jnp.float32)
         scale = jnp.where(bit == 31, -(2.0**-31), power * 2.0**-30)
@@ -284,21 +286,18 @@
     device = lax.broadcast(lax.axis_index("device"), (1, BLOCK))
     for row, values in enumerate((pre_block, block_mask, delay, device), 8):
         first_input = jnp.where(row_ids(16) == row, values, first_input)
-    copies, early_plan, late_plan = kernel_call(
-        first_body,
-        (words, codes, codes),
-        [VMEM],
-        [],
-        "first",
-        8,
-        pl.CostEstimate(flops=10**10, bytes_accessed=1 << 18, transcendentals=0),
-    )(first_input)
+    cost = pl.CostEstimate(flops=10**10, bytes_accessed=1 << 18, transcendentals=0)
+    copies = kernel_call(first_body, words, [VMEM], [], "first", 8, cost)(first_input)
     own, other = [], []
     devices = range(lax.axis_size("device"))
-    chips = [sorted((d for d in devices if d // CORE % 2 == c), key=chip_order) for c in range(2)]
+    teams = [sorted((d for d in devices if team(d) == t), key=place) for t in range(2)]
     for number in range(STEPS // DMIN):
-        mine = exchanged(copies, chips)
+        mine = exchanged(copies, teams)
         theirs = lax.ppermute(mine, "device", [(d, d ^ CORE) for d in devices])
+        if number == 0:
+            early_plan, late_plan = kernel_call(
+                plan_body, (codes, codes), [VMEM, ANY], [], "plan", 8
+            )(first_input, mine)
         own = [mine] + own[:2]
         n_hist = len(own)
         early = kernel_call(

time: 141 us -> 141 us (level)
  starting transfers between devices: 0.01 us -> 2.11 us
  blocking collectives: 126 us -> 124 us
    ppermute x5, starting transfers between devices: 0.01 us -> 2.11 us  [on_device(): theirs = lax.ppermute(mine, 'device', [(d, d ^ CORE) for d in devices])]
    all_to_all x6, blocking collectives: 126 us -> 124 us  [exchanged(): lax.all_to_all(pieces, 'device', split_axis=0, concat_axis=0, axis_index_...]
  transfers between devices with their start and end apart: 5 -> 5, of which waited for: 5 -> 0; matrix products, arithmetic and copies ran while one was open for 0% -> 0% of each run, Pallas kernels for 4% -> 5%
where the time goes in v6:
time: 141 us; the launch traced here: 139 us
  blocking collectives  124 us (88%)
  Pallas kernels  10.5 us (7%)
  starting transfers between devices  2.11 us (1%)
    all_to_all x6, blocking collectives, exchanged(): lax.all_to_all(pieces, 'device', split_axis=0, concat_axis=0, axis_index_...  124 us
    pallas_call x5, Pallas kernels, on_device(): kernel_call(early_body(n_hist), sums, [VMEM] + [VMEM] * (2 * n_hist), [ta...  6.05 us
    pallas_call x5, Pallas kernels, on_device(): kernel_call(late_body(number, n_hist), (volts, out) if last else (volts,...  3.16 us
  transfers between devices with their start and end apart: 5, of which 0 were waited for; matrix products, arithmetic and copies ran while one was open for 0% of the time, Pallas kernels for 5%

profile of v6, /device:TPU:32, one launch (start us, length us, event | category | flops | bytes accessed | tf_op | source)
XLA Modules:
  0.0 138.7 jit_solution(8171058668208950074)
XLA Ops:
  0.7 0.8 select_select_fusion.input_ref
  1.5 0.0 copy-start
  1.5 0.2 first.1
  1.6 0.0 copy-start.1
  1.7 0.0 copy-start.2
  1.7 0.0 copy-start.3
  1.7 27.6 %all_to_all.30 = s32[128,1,384]{2,1,0:T(1,128)S(1)} all-to-all(s32[128,1,384]{2,1,0:T(1,128)S(1)} %bitcast.57), channel_id=1, replica_groups={{9,65,137,193,2,74,130,202,11,67,139,195,4,76,132,204,13,69,141,197,6,7..., dimensions={0} | all-to-all | bytes 393216 | tf_op jit(solution)/shard_map/all_to_all | solution.py:262
  29.3 0.6 collective-permute-start
  29.8 0.3 plan.1
  30.2 0.0 copy-done
  30.2 1.2 early.5.refs_2_
  31.4 0.0 collective-permute-done.refs_0_.refs_2_.refs_1_.refs_4_
  31.4 0.0 copy-done.1
  31.4 0.0 copy-done.2
  31.4 0.0 copy-done.3
  31.4 0.6 late.5
  32.0 19.7 %all_to_all.31 = s32[128,1,384]{2,1,0:T(1,128)S(1)} all-to-all(s32[128,1,384]{2,1,0:T(1,128)S(1)} %bitcast.56), channel_id=1, replica_groups={{9,65,137,193,2,74,130,202,11,67,139,195,4,76,132,204,13,69,141,197,6,7..., dimensions={0} | all-to-all | bytes 393216 | tf_op jit(solution)/shard_map/all_to_all | solution.py:262
  51.7 0.2 collective-permute-start.1
  51.9 1.2 early.6.refs_3_
  53.1 0.0 collective-permute-done.1.refs_0_.refs_3_.refs_1_.refs_4_
  53.1 0.6 late.6
  53.8 19.5 %all_to_all.32 = s32[128,1,384]{2,1,0:T(1,128)S(1)} all-to-all(s32[128,1,384]{2,1,0:T(1,128)S(1)} %bitcast.53), channel_id=1, replica_groups={{9,65,137,193,2,74,130,202,11,67,139,195,4,76,132,204,13,69,141,197,6,7..., dimensions={0} | all-to-all | bytes 393216 | tf_op jit(solution)/shard_map/all_to_all | solution.py:262
  73.3 0.4 collective-permute-start.2
  73.7 1.2 early.7.refs_3_
  75.0 0.0 collective-permute-done.2.refs_0_.refs_3_.refs_1_.refs_4_
  75.0 0.6 late.7
  75.6 19.3 %all_to_all.33 = s32[128,1,384]{2,1,0:T(1,128)S(1)} all-to-all(s32[128,1,384]{2,1,0:T(1,128)S(1)} %bitcast.54), channel_id=1, replica_groups={{9,65,137,193,2,74,130,202,11,67,139,195,4,76,132,204,13,69,141,197,6,7..., dimensions={0} | all-to-all | bytes 393216 | tf_op jit(solution)/shard_map/all_to_all | solution.py:262
  94.9 0.4 collective-permute-start.3
  95.3 1.2 early.8.refs_3_
  96.6 0.0 collective-permute-done.3.refs_0_.refs_3_.refs_1_
  96.6 0.6 late.8
  97.2 19.3 %all_to_all.34 = s32[128,1,384]{2,1,0:T(1,128)S(1)} all-to-all(s32[128,1,384]{2,1,0:T(1,128)S(1)} %bitcast.55), channel_id=1, replica_groups={{9,65,137,193,2,74,130,202,11,67,139,195,4,76,132,204,13,69,141,197,6,7..., dimensions={0} | all-to-all | bytes 393216 | tf_op jit(solution)/shard_map/all_to_all | solution.py:262
  116.5 0.0 copy-start.4
  116.5 0.5 collective-permute-start.4
  117.0 1.2 early.9.refs_3_
  118.2 0.0 collective-permute-done.4.refs_0_
  118.2 0.7 late.9
  118.9 19.0 %all_to_all.35 = f32[256,1,128]{2,1,0:T(1,128)S(1)} all-to-all(f32[256,1,128]{2,1,0:T(1,128)S(1)} %bitcast.58), channel_id=1, replica_groups={{0,1,2,3,4,5,6,7,8,9,10,11,12,13,14,15,16,17,18,19,20,21,22,23,24,25,26..., dimensions={0} | all-to-all | bytes 262144 | tf_op jit(solution)/shard_map/all_to_all | solution.py:262
  137.9 0.0 copy-done.4
  137.9 0.8 rates.1
  (2 shorter events, 0.0 us)
Async XLA Ops:
  1.5 28.7 %copy-start = (bf16[1,128,128,128]{3,2,1,0:T(8,128)(2,1)S(1)}, bf16[1,128,128,128]{3,2,1,0:T(8,128)(2,1)}, u32[]{:S(2)}) copy-start(bf16[1,128,128,128]{3,2,1,0:T(8,128)(2,1)} %param.13) | copy-start | bytes 12582916
  1.6 29.7 %copy-start.1 = (f32[48,128]{1,0:T(8,128)S(1)}, f32[48,128]{1,0:T(8,128)}, u32[]{:S(2)}) copy-start(f32[48,128]{1,0:T(8,128)} %refs_3_.1) | copy-start | bytes 73732
  1.7 29.7 %copy-start.2 = (s32[128]{0:T(128)S(1)}, s32[128]{0:T(128)}, u32[]{:S(2)}) copy-start(s32[128]{0:T(128)} %param.11) | copy-start | bytes 1540
  1.7 29.7 %copy-start.3 = (s32[128]{0:T(128)S(1)}, s32[128]{0:T(128)}, u32[]{:S(2)}) copy-start(s32[128]{0:T(128)} %param.12) | copy-start | bytes 1540
  29.3 2.1 %collective-permute-start = (s32[384,128]{1,0:T(8,128)S(1)}, s32[384,128]{1,0:T(8,128)S(1)}, u32[]{:S(2)}, u32[]{:S(2)}) collective-permute-start(s32[384,128]{1,0:T(8,128)S(1)} %bitcast.34), channel_id=1, source_target_pairs={{0,8},{1,9},{2,10},{3,11},{4,12},{5,13},{6,14},{7,15},{8,0},{9,1},... | collective-permute-start | bytes 589832 | tf_op jit(solution)/shard_map/ppermute | solution.py:296
  51.7 1.4 %collective-permute-start.1 = (s32[384,128]{1,0:T(8,128)S(1)}, s32[384,128]{1,0:T(8,128)S(1)}, u32[]{:S(2)}, u32[]{:S(2)}) collective-permute-start(s32[384,128]{1,0:T(8,128)S(1)} %bitcast.39), channel_id=1, source_target_pairs={{0,8},{1,9},{2,10},{3,11},{4,12},{5,13},{6,14},{7,15},{8,0},{9,1},... | collective-permute-start | bytes 589832 | tf_op jit(solution)/shard_map/ppermute | solution.py:296
  73.3 1.7 %collective-permute-start.2 = (s32[384,128]{1,0:T(8,128)S(1)}, s32[384,128]{1,0:T(8,128)S(1)}, u32[]{:S(2)}, u32[]{:S(2)}) collective-permute-start(s32[384,128]{1,0:T(8,128)S(1)} %bitcast.43), channel_id=1, source_target_pairs={{0,8},{1,9},{2,10},{3,11},{4,12},{5,13},{6,14},{7,15},{8,0},{9,1},... | collective-permute-start | bytes 589832 | tf_op jit(solution)/shard_map/ppermute | solution.py:296
  94.9 1.7 %collective-permute-start.3 = (s32[384,128]{1,0:T(8,128)S(1)}, s32[384,128]{1,0:T(8,128)S(1)}, u32[]{:S(2)}, u32[]{:S(2)}) collective-permute-start(s32[384,128]{1,0:T(8,128)S(1)} %bitcast.47), channel_id=1, source_target_pairs={{0,8},{1,9},{2,10},{3,11},{4,12},{5,13},{6,14},{7,15},{8,0},{9,1},... | collective-permute-start | bytes 589832 | tf_op jit(solution)/shard_map/ppermute | solution.py:296
  116.5 21.4 %copy-start.4 = (s32[256,1]{0,1:T(1,128)S(1)}, s32[256,1]{0,1:T(1,128)}, u32[]{:S(2)}) copy-start(s32[256,1]{0,1:T(1,128)} %param.17) | copy-start | bytes 3076
  116.5 1.7 %collective-permute-start.4 = (s32[384,128]{1,0:T(8,128)S(1)}, s32[384,128]{1,0:T(8,128)S(1)}, u32[]{:S(2)}, u32[]{:S(2)}) collective-permute-start(s32[384,128]{1,0:T(8,128)S(1)} %bitcast.50), channel_id=1, source_target_pairs={{0,8},{1,9},{2,10},{3,11},{4,12},{5,13},{6,14},{7,15},{8,0},{9,1},... | collective-permute-start | bytes 589832 | tf_op jit(solution)/shard_map/ppermute | solution.py:296

commit v7 on v6

--- a/solution.py
+++ b/solution.py
@@ -87,12 +87,11 @@
 
 
 def team(block):
-    return (block // 64 + block // 16 + block + block // CORE) % 2
+    return (block // 32 + block // CORE) % 2
 
 
 def place(block):
-    z = (block + 7 + team(block)) % 8
-    return (block // 16 % 4 * 8 + z) * 4 + block // 64
+    return (block // 16 % 4 * 8 + block % 8) * 4 + block // 64
 
 
 def slot_codes(pre, mask, delay, device):

time: 141 us -> 142 us (level)
  starting transfers between devices: 2.11 us -> 4.51 us
    ppermute x5, starting transfers between devices: 2.11 us -> 4.51 us  [on_device(): theirs = lax.ppermute(mine, 'device', [(d, d ^ CORE) for d in devices])]
where the time goes in v7:
time: 142 us; the launch traced here: 140 us
  blocking collectives  123 us (87%)
  Pallas kernels  10.6 us (7%)
  starting transfers between devices  4.51 us (3%)
    all_to_all x6, blocking collectives, exchanged(): lax.all_to_all(pieces, 'device', split_axis=0, concat_axis=0, axis_index_...  123 us
    pallas_call x5, Pallas kernels, on_device(): kernel_call(early_body(n_hist), sums, [VMEM] + [VMEM] * (2 * n_hist), [ta...  6.09 us
    ppermute x5, starting transfers between devices, on_device(): theirs = lax.ppermute(mine, 'device', [(d, d ^ CORE) for d in devices])  4.51 us
    pallas_call x5, Pallas kernels, on_device(): kernel_call(late_body(number, n_hist), (volts, out) if last else (volts,...  3.17 us
  transfers between devices with their start and end apart: 5, of which 0 were waited for; matrix products, arithmetic and copies ran while one was open for 0% of the time, Pallas kernels for 5%

profile of v7, /device:TPU:32, one launch (start us, length us, event | category | flops | bytes accessed | tf_op | source)
XLA Modules:
  0.0 139.7 jit_solution(8645296330769250853)
XLA Ops:
  0.7 0.8 select_select_fusion.input_ref
  1.5 0.0 copy-start
  1.5 0.2 first.1
  1.6 0.0 copy-start.1
  1.7 0.0 copy-start.2
  1.7 0.0 copy-start.3
  1.7 27.0 %all_to_all.30 = s32[128,1,384]{2,1,0:T(1,128)S(1)} all-to-all(s32[128,1,384]{2,1,0:T(1,128)S(1)} %bitcast.57), channel_id=1, replica_groups={{0,64,128,192,1,65,129,193,2,66,130,194,3,67,131,195,4,68,132,196,5,69,..., dimensions={0} | all-to-all | bytes 393216 | tf_op jit(solution)/shard_map/all_to_all | solution.py:261
  28.6 1.2 collective-permute-start
  29.8 0.3 plan.1
  30.2 0.0 copy-done
  30.2 1.2 early.5.refs_2_
  31.4 0.0 collective-permute-done.refs_0_.refs_2_.refs_1_.refs_4_
  31.4 0.0 copy-done.1
  31.4 0.0 copy-done.2
  31.4 0.0 copy-done.3
  31.4 0.6 late.5
  32.0 19.3 %all_to_all.31 = s32[128,1,384]{2,1,0:T(1,128)S(1)} all-to-all(s32[128,1,384]{2,1,0:T(1,128)S(1)} %bitcast.56), channel_id=1, replica_groups={{0,64,128,192,1,65,129,193,2,66,130,194,3,67,131,195,4,68,132,196,5,69,..., dimensions={0} | all-to-all | bytes 393216 | tf_op jit(solution)/shard_map/all_to_all | solution.py:261
  51.3 0.7 collective-permute-start.1
  52.0 1.2 early.6.refs_3_
  53.2 0.0 collective-permute-done.1.refs_0_.refs_3_.refs_1_.refs_4_
  53.2 0.6 late.6
  53.9 19.4 %all_to_all.32 = s32[128,1,384]{2,1,0:T(1,128)S(1)} all-to-all(s32[128,1,384]{2,1,0:T(1,128)S(1)} %bitcast.53), channel_id=1, replica_groups={{0,64,128,192,1,65,129,193,2,66,130,194,3,67,131,195,4,68,132,196,5,69,..., dimensions={0} | all-to-all | bytes 393216 | tf_op jit(solution)/shard_map/all_to_all | solution.py:261
  73.2 0.9 collective-permute-start.2
  74.1 1.2 early.7.refs_3_
  75.4 0.0 collective-permute-done.2.refs_0_.refs_3_.refs_1_.refs_4_
  75.4 0.6 late.7
  76.0 19.3 %all_to_all.33 = s32[128,1,384]{2,1,0:T(1,128)S(1)} all-to-all(s32[128,1,384]{2,1,0:T(1,128)S(1)} %bitcast.54), channel_id=1, replica_groups={{0,64,128,192,1,65,129,193,2,66,130,194,3,67,131,195,4,68,132,196,5,69,..., dimensions={0} | all-to-all | bytes 393216 | tf_op jit(solution)/shard_map/all_to_all | solution.py:261
  95.3 0.9 collective-permute-start.3
  96.1 1.2 early.8.refs_3_
  97.4 0.0 collective-permute-done.3.refs_0_.refs_3_.refs_1_
  97.4 0.6 late.8
  98.0 19.3 %all_to_all.34 = s32[128,1,384]{2,1,0:T(1,128)S(1)} all-to-all(s32[128,1,384]{2,1,0:T(1,128)S(1)} %bitcast.55), channel_id=1, replica_groups={{0,64,128,192,1,65,129,193,2,66,130,194,3,67,131,195,4,68,132,196,5,69,..., dimensions={0} | all-to-all | bytes 393216 | tf_op jit(solution)/shard_map/all_to_all | solution.py:261
  117.3 0.0 copy-start.4
  117.3 0.9 collective-permute-start.4
  118.2 1.2 early.9.refs_3_
  119.4 0.0 collective-permute-done.4.refs_0_
  119.4 0.7 late.9
  120.1 18.8 %all_to_all.35 = f32[256,1,128]{2,1,0:T(1,128)S(1)} all-to-all(f32[256,1,128]{2,1,0:T(1,128)S(1)} %bitcast.58), channel_id=1, replica_groups={{0,1,2,3,4,5,6,7,8,9,10,11,12,13,14,15,16,17,18,19,20,21,22,23,24,25,26..., dimensions={0} | all-to-all | bytes 262144 | tf_op jit(solution)/shard_map/all_to_all | solution.py:261
  138.9 0.0 copy-done.4
  138.9 0.8 rates.1
  (2 shorter events, 0.0 us)
Async XLA Ops:
  1.5 28.7 %copy-start = (bf16[1,128,128,128]{3,2,1,0:T(8,128)(2,1)S(1)}, bf16[1,128,128,128]{3,2,1,0:T(8,128)(2,1)}, u32[]{:S(2)}) copy-start(bf16[1,128,128,128]{3,2,1,0:T(8,128)(2,1)} %param.13) | copy-start | bytes 12582916
  1.6 29.7 %copy-start.1 = (f32[48,128]{1,0:T(8,128)S(1)}, f32[48,128]{1,0:T(8,128)}, u32[]{:S(2)}) copy-start(f32[48,128]{1,0:T(8,128)} %refs_3_.1) | copy-start | bytes 73732
  1.7 29.7 %copy-start.2 = (s32[128]{0:T(128)S(1)}, s32[128]{0:T(128)}, u32[]{:S(2)}) copy-start(s32[128]{0:T(128)} %param.11) | copy-start | bytes 1540
  1.7 29.7 %copy-start.3 = (s32[128]{0:T(128)S(1)}, s32[128]{0:T(128)}, u32[]{:S(2)}) copy-start(s32[128]{0:T(128)} %param.12) | copy-start | bytes 1540
  28.6 2.7 %collective-permute-start = (s32[384,128]{1,0:T(8,128)S(1)}, s32[384,128]{1,0:T(8,128)S(1)}, u32[]{:S(2)}, u32[]{:S(2)}) collective-permute-start(s32[384,128]{1,0:T(8,128)S(1)} %bitcast.34), channel_id=1, source_target_pairs={{0,8},{1,9},{2,10},{3,11},{4,12},{5,13},{6,14},{7,15},{8,0},{9,1},... | collective-permute-start | bytes 589832 | tf_op jit(solution)/shard_map/ppermute | solution.py:295
  51.3 1.9 %collective-permute-start.1 = (s32[384,128]{1,0:T(8,128)S(1)}, s32[384,128]{1,0:T(8,128)S(1)}, u32[]{:S(2)}, u32[]{:S(2)}) collective-permute-start(s32[384,128]{1,0:T(8,128)S(1)} %bitcast.39), channel_id=1, source_target_pairs={{0,8},{1,9},{2,10},{3,11},{4,12},{5,13},{6,14},{7,15},{8,0},{9,1},... | collective-permute-start | bytes 589832 | tf_op jit(solution)/shard_map/ppermute | solution.py:295
  73.2 2.2 %collective-permute-start.2 = (s32[384,128]{1,0:T(8,128)S(1)}, s32[384,128]{1,0:T(8,128)S(1)}, u32[]{:S(2)}, u32[]{:S(2)}) collective-permute-start(s32[384,128]{1,0:T(8,128)S(1)} %bitcast.43), channel_id=1, source_target_pairs={{0,8},{1,9},{2,10},{3,11},{4,12},{5,13},{6,14},{7,15},{8,0},{9,1},... | collective-permute-start | bytes 589832 | tf_op jit(solution)/shard_map/ppermute | solution.py:295
  95.3 2.1 %collective-permute-start.3 = (s32[384,128]{1,0:T(8,128)S(1)}, s32[384,128]{1,0:T(8,128)S(1)}, u32[]{:S(2)}, u32[]{:S(2)}) collective-permute-start(s32[384,128]{1,0:T(8,128)S(1)} %bitcast.47), channel_id=1, source_target_pairs={{0,8},{1,9},{2,10},{3,11},{4,12},{5,13},{6,14},{7,15},{8,0},{9,1},... | collective-permute-start | bytes 589832 | tf_op jit(solution)/shard_map/ppermute | solution.py:295
  117.3 21.6 %copy-start.4 = (s32[256,1]{0,1:T(1,128)S(1)}, s32[256,1]{0,1:T(1,128)}, u32[]{:S(2)}) copy-start(s32[256,1]{0,1:T(1,128)} %param.17) | copy-start | bytes 3076
  117.3 2.1 %collective-permute-start.4 = (s32[384,128]{1,0:T(8,128)S(1)}, s32[384,128]{1,0:T(8,128)S(1)}, u32[]{:S(2)}, u32[]{:S(2)}) collective-permute-start(s32[384,128]{1,0:T(8,128)S(1)} %bitcast.50), channel_id=1, source_target_pairs={{0,8},{1,9},{2,10},{3,11},{4,12},{5,13},{6,14},{7,15},{8,0},{9,1},... | collective-permute-start | bytes 589832 | tf_op jit(solution)/shard_map/ppermute | solution.py:295

commit v8 on v7

--- a/solution.py
+++ b/solution.py
@@ -87,11 +87,19 @@
 
 
 def team(block):
-    return (block // 32 + block // CORE) % 2
+    return block // CORE % 2
+
+
+def chip_key(block):
+    y, x, z = block // 64, block // 16 % 4, block % 8
+    hops = y - 2 * (y // 3) + x - 2 * (x // 3) + z - z // 4 * (2 * z - 8)
+    return (9 - hops) % 9 * 128 + (y * 8 + z) * 4 + x
 
 
 def place(block):
-    return (block // 16 % 4 * 8 + block % 8) * 4 + block // 64
+    chip = row_ids(128)
+    keys = chip_key(chip // 8 * 16 + chip % 8)
+    return jnp.sum((keys < chip_key(block)).astype(jnp.int32), axis=0, keepdims=True, dtype=jnp.int32)
 
 
 def slot_codes(pre, mask, delay, device):
@@ -289,7 +297,7 @@
     copies = kernel_call(first_body, words, [VMEM], [], "first", 8, cost)(first_input)
     own, other = [], []
     devices = range(lax.axis_size("device"))
-    teams = [sorted((d for d in devices if team(d) == t), key=place) for t in range(2)]
+    teams = [sorted((d for d in devices if team(d) == t), key=chip_key) for t in range(2)]
     for number in range(STEPS // DMIN):
         mine = exchanged(copies, teams)
         theirs = lax.ppermute(mine, "device", [(d, d ^ CORE) for d in devices])

time: 142 us -> 139 us (0.979)
  starting transfers between devices: 4.51 us -> 0.01 us
    ppermute x5, starting transfers between devices: 4.51 us -> 0.01 us  [on_device(): theirs = lax.ppermute(mine, 'device', [(d, d ^ CORE) for d in devices])]
  transfers between devices with their start and end apart: 5 -> 5, of which waited for: 0 -> 4; matrix products, arithmetic and copies ran while one was open for 0% -> 0% of each run, Pallas kernels for 5% -> 5%
where the time goes in v8:
time: 139 us; the launch traced here: 137 us
  blocking collectives  124 us (89%)
  Pallas kernels  10.9 us (8%)
    all_to_all x6, blocking collectives, exchanged(): lax.all_to_all(pieces, 'device', split_axis=0, concat_axis=0, axis_index_...  124 us
    pallas_call x5, Pallas kernels, on_device(): kernel_call(early_body(n_hist), sums, [VMEM] + [VMEM] * (2 * n_hist), [ta...  6.07 us
    pallas_call x5, Pallas kernels, on_device(): kernel_call(late_body(number, n_hist), (volts, out) if last else (volts,...  3.12 us
  transfers between devices with their start and end apart: 5, of which 4 were waited for; matrix products, arithmetic and copies ran while one was open for 0% of the time, Pallas kernels for 5%

profile of v8, /device:TPU:32, one launch (start us, length us, event | category | flops | bytes accessed | tf_op | source)
XLA Modules:
  0.0 137.3 jit_solution(4881488133850216041)
XLA Ops:
  0.7 0.8 select_select_fusion.input_ref
  1.5 0.0 copy-start
  1.5 0.2 first.1
  1.6 0.0 copy-start.1
  1.7 0.0 copy-start.2
  1.7 0.0 copy-start.3
  1.7 28.0 %all_to_all.30 = s32[128,1,384]{2,1,0:T(1,128)S(1)} all-to-all(s32[128,1,384]{2,1,0:T(1,128)S(1)} %bitcast.57), channel_id=1, replica_groups={{0,164,100,163,148,180,165,228,36,99,84,116,101,162,147,179,132,149,181..., dimensions={0} | all-to-all | bytes 393216 | tf_op jit(solution)/shard_map/all_to_all | solution.py:269
  29.7 0.0 collective-permute-start
  29.7 0.7 plan.1
  30.4 0.0 copy-done
  30.4 1.2 early.5.refs_2_
  31.6 0.0 collective-permute-done.refs_0_.refs_2_.refs_1_.refs_4_
  31.6 0.0 copy-done.1
  31.6 0.0 copy-done.2
  31.6 0.0 copy-done.3
  31.6 0.6 late.5
  32.3 19.6 %all_to_all.31 = s32[128,1,384]{2,1,0:T(1,128)S(1)} all-to-all(s32[128,1,384]{2,1,0:T(1,128)S(1)} %bitcast.56), channel_id=1, replica_groups={{0,164,100,163,148,180,165,228,36,99,84,116,101,162,147,179,132,149,181..., dimensions={0} | all-to-all | bytes 393216 | tf_op jit(solution)/shard_map/all_to_all | solution.py:269
  51.8 0.0 collective-permute-start.1
  51.8 1.2 early.6.refs_3_
  53.0 0.2 collective-permute-done.1.refs_0_.refs_3_.refs_1_.refs_4_
  53.3 0.6 late.6
  53.9 19.3 %all_to_all.32 = s32[128,1,384]{2,1,0:T(1,128)S(1)} all-to-all(s32[128,1,384]{2,1,0:T(1,128)S(1)} %bitcast.53), channel_id=1, replica_groups={{0,164,100,163,148,180,165,228,36,99,84,116,101,162,147,179,132,149,181..., dimensions={0} | all-to-all | bytes 393216 | tf_op jit(solution)/shard_map/all_to_all | solution.py:269
  73.2 0.0 collective-permute-start.2
  73.2 1.2 early.7.refs_3_
  74.4 0.2 collective-permute-done.2.refs_0_.refs_3_.refs_1_.refs_4_
  74.6 0.6 late.7
  75.3 19.5 %all_to_all.33 = s32[128,1,384]{2,1,0:T(1,128)S(1)} all-to-all(s32[128,1,384]{2,1,0:T(1,128)S(1)} %bitcast.54), channel_id=1, replica_groups={{0,164,100,163,148,180,165,228,36,99,84,116,101,162,147,179,132,149,181..., dimensions={0} | all-to-all | bytes 393216 | tf_op jit(solution)/shard_map/all_to_all | solution.py:269
  94.8 0.0 collective-permute-start.3
  94.8 1.2 early.8.refs_3_
  96.0 0.2 collective-permute-done.3.refs_0_.refs_3_.refs_1_
  96.2 0.6 late.8
  96.8 19.4 %all_to_all.34 = s32[128,1,384]{2,1,0:T(1,128)S(1)} all-to-all(s32[128,1,384]{2,1,0:T(1,128)S(1)} %bitcast.55), channel_id=1, replica_groups={{0,164,100,163,148,180,165,228,36,99,84,116,101,162,147,179,132,149,181..., dimensions={0} | all-to-all | bytes 393216 | tf_op jit(solution)/shard_map/all_to_all | solution.py:269
  116.2 0.0 copy-start.4
  116.2 0.0 collective-permute-start.4
  116.2 1.2 early.9.refs_3_
  117.4 0.2 collective-permute-done.4.refs_0_
  117.6 0.7 late.9
  118.3 18.2 %all_to_all.35 = f32[256,1,128]{2,1,0:T(1,128)S(1)} all-to-all(f32[256,1,128]{2,1,0:T(1,128)S(1)} %bitcast.58), channel_id=1, replica_groups={{0,1,2,3,4,5,6,7,8,9,10,11,12,13,14,15,16,17,18,19,20,21,22,23,24,25,26..., dimensions={0} | all-to-all | bytes 262144 | tf_op jit(solution)/shard_map/all_to_all | solution.py:269
  136.5 0.0 copy-done.4
  136.5 0.8 rates.1
  (2 shorter events, 0.0 us)
Async XLA Ops:
  1.5 28.9 %copy-start = (bf16[1,128,128,128]{3,2,1,0:T(8,128)(2,1)S(1)}, bf16[1,128,128,128]{3,2,1,0:T(8,128)(2,1)}, u32[]{:S(2)}) copy-start(bf16[1,128,128,128]{3,2,1,0:T(8,128)(2,1)} %param.13) | copy-start | bytes 12582916
  1.6 30.0 %copy-start.1 = (f32[48,128]{1,0:T(8,128)S(1)}, f32[48,128]{1,0:T(8,128)}, u32[]{:S(2)}) copy-start(f32[48,128]{1,0:T(8,128)} %refs_3_.1) | copy-start | bytes 73732
  1.7 30.0 %copy-start.2 = (s32[128]{0:T(128)S(1)}, s32[128]{0:T(128)}, u32[]{:S(2)}) copy-start(s32[128]{0:T(128)} %param.11) | copy-start | bytes 1540
  1.7 30.0 %copy-start.3 = (s32[128]{0:T(128)S(1)}, s32[128]{0:T(128)}, u32[]{:S(2)}) copy-start(s32[128]{0:T(128)} %param.12) | copy-start | bytes 1540
  29.7 1.9 %collective-permute-start = (s32[384,128]{1,0:T(8,128)S(1)}, s32[384,128]{1,0:T(8,128)S(1)}, u32[]{:S(2)}, u32[]{:S(2)}) collective-permute-start(s32[384,128]{1,0:T(8,128)S(1)} %bitcast.34), channel_id=1, source_target_pairs={{0,8},{1,9},{2,10},{3,11},{4,12},{5,13},{6,14},{7,15},{8,0},{9,1},... | collective-permute-start | bytes 589832 | tf_op jit(solution)/shard_map/ppermute | solution.py:303
  51.8 1.4 %collective-permute-start.1 = (s32[384,128]{1,0:T(8,128)S(1)}, s32[384,128]{1,0:T(8,128)S(1)}, u32[]{:S(2)}, u32[]{:S(2)}) collective-permute-start(s32[384,128]{1,0:T(8,128)S(1)} %bitcast.39), channel_id=1, source_target_pairs={{0,8},{1,9},{2,10},{3,11},{4,12},{5,13},{6,14},{7,15},{8,0},{9,1},... | collective-permute-start | bytes 589832 | tf_op jit(solution)/shard_map/ppermute | solution.py:303
  73.2 1.4 %collective-permute-start.2 = (s32[384,128]{1,0:T(8,128)S(1)}, s32[384,128]{1,0:T(8,128)S(1)}, u32[]{:S(2)}, u32[]{:S(2)}) collective-permute-start(s32[384,128]{1,0:T(8,128)S(1)} %bitcast.43), channel_id=1, source_target_pairs={{0,8},{1,9},{2,10},{3,11},{4,12},{5,13},{6,14},{7,15},{8,0},{9,1},... | collective-permute-start | bytes 589832 | tf_op jit(solution)/shard_map/ppermute | solution.py:303
  94.8 1.4 %collective-permute-start.3 = (s32[384,128]{1,0:T(8,128)S(1)}, s32[384,128]{1,0:T(8,128)S(1)}, u32[]{:S(2)}, u32[]{:S(2)}) collective-permute-start(s32[384,128]{1,0:T(8,128)S(1)} %bitcast.47), channel_id=1, source_target_pairs={{0,8},{1,9},{2,10},{3,11},{4,12},{5,13},{6,14},{7,15},{8,0},{9,1},... | collective-permute-start | bytes 589832 | tf_op jit(solution)/shard_map/ppermute | solution.py:303
  116.2 20.3 %copy-start.4 = (s32[256,1]{0,1:T(1,128)S(1)}, s32[256,1]{0,1:T(1,128)}, u32[]{:S(2)}) copy-start(s32[256,1]{0,1:T(1,128)} %param.17) | copy-start | bytes 3076
  116.2 1.4 %collective-permute-start.4 = (s32[384,128]{1,0:T(8,128)S(1)}, s32[384,128]{1,0:T(8,128)S(1)}, u32[]{:S(2)}, u32[]{:S(2)}) collective-permute-start(s32[384,128]{1,0:T(8,128)S(1)} %bitcast.50), channel_id=1, source_target_pairs={{0,8},{1,9},{2,10},{3,11},{4,12},{5,13},{6,14},{7,15},{8,0},{9,1},... | collective-permute-start | bytes 589832 | tf_op jit(solution)/shard_map/ppermute | solution.py:303

commit v9 on v8

--- a/solution.py
+++ b/solution.py
@@ -96,9 +96,13 @@
     return (9 - hops) % 9 * 128 + (y * 8 + z) * 4 + x
 
 
+def column(row):
+    return jnp.transpose(jnp.broadcast_to(row, (BLOCK, BLOCK)))
+
+
 def place(block):
-    chip = row_ids(128)
-    keys = chip_key(chip // 8 * 16 + chip % 8)
+    chip = lane_ids(1)
+    keys = column(chip_key(chip // 8 * 16 + chip % 8))
     return jnp.sum((keys < chip_key(block)).astype(jnp.int32), axis=0, keepdims=True, dtype=jnp.int32)
 
 
@@ -116,7 +120,7 @@
     kind = jnp.broadcast_to(jnp.right_shift(slots, 20), (SLOTS, SLOTS))
     code = jnp.bitwise_and(slots, (1 << 20) - 1)
     sub, lane = row_ids(SLOTS), lane_ids(SLOTS)
-    before = jnp.where((jnp.transpose(kind) == kind) & (sub < lane), 1, 0)
+    before = jnp.where((column(kind[:1]) == kind) & (sub < lane), 1, 0)
     rank = jnp.sum(before, axis=0, keepdims=True, dtype=jnp.int32)
     nothing = NDELAY * TABLE * SLOTS
     for k, out_ref in enumerate(out_refs):

time: 139 us -> 139 us (level)
  no operation moved by 1% of the time
where the time goes in v9:
time: 139 us; the launch traced here: 137 us
  blocking collectives  124 us (89%)
  Pallas kernels  10.7 us (8%)
    all_to_all x6, blocking collectives, exchanged(): lax.all_to_all(pieces, 'device', split_axis=0, concat_axis=0, axis_index_...  124 us
    pallas_call x5, Pallas kernels, on_device(): kernel_call(early_body(n_hist), sums, [VMEM] + [VMEM] * (2 * n_hist), [ta...  6.08 us
    pallas_call x5, Pallas kernels, on_device(): kernel_call(late_body(number, n_hist), (volts, out) if last else (volts,...  3.14 us
  transfers between devices with their start and end apart: 5, of which 4 were waited for; matrix products, arithmetic and copies ran while one was open for 0% of the time, Pallas kernels for 5%

profile of v9, /device:TPU:32, one launch (start us, length us, event | category | flops | bytes accessed | tf_op | source)
XLA Modules:
  0.0 137.1 jit_solution(17730213476432444163)
XLA Ops:
  0.7 0.8 select_select_fusion.input_ref
  1.5 0.0 copy-start
  1.5 0.2 first.1
  1.6 0.0 copy-start.1
  1.7 0.0 copy-start.2
  1.7 0.0 copy-start.3
  1.7 28.0 %all_to_all.30 = s32[128,1,384]{2,1,0:T(1,128)S(1)} all-to-all(s32[128,1,384]{2,1,0:T(1,128)S(1)} %bitcast.57), channel_id=1, replica_groups={{0,164,100,163,148,180,165,228,36,99,84,116,101,162,147,179,132,149,181..., dimensions={0} | all-to-all | bytes 393216 | tf_op jit(solution)/shard_map/all_to_all | solution.py:273
  29.7 0.0 collective-permute-start
  29.7 0.5 plan.1
  30.1 0.0 copy-done
  30.2 1.2 early.5.refs_2_
  31.4 0.0 collective-permute-done.refs_0_.refs_2_.refs_1_.refs_4_
  31.4 0.0 copy-done.1
  31.4 0.0 copy-done.2
  31.4 0.0 copy-done.3
  31.4 0.6 late.5
  32.0 19.6 %all_to_all.31 = s32[128,1,384]{2,1,0:T(1,128)S(1)} all-to-all(s32[128,1,384]{2,1,0:T(1,128)S(1)} %bitcast.56), channel_id=1, replica_groups={{0,164,100,163,148,180,165,228,36,99,84,116,101,162,147,179,132,149,181..., dimensions={0} | all-to-all | bytes 393216 | tf_op jit(solution)/shard_map/all_to_all | solution.py:273
  51.6 0.0 collective-permute-start.1
  51.6 1.2 early.6.refs_3_
  52.8 0.2 collective-permute-done.1.refs_0_.refs_3_.refs_1_.refs_4_
  53.0 0.6 late.6
  53.6 19.3 %all_to_all.32 = s32[128,1,384]{2,1,0:T(1,128)S(1)} all-to-all(s32[128,1,384]{2,1,0:T(1,128)S(1)} %bitcast.53), channel_id=1, replica_groups={{0,164,100,163,148,180,165,228,36,99,84,116,101,162,147,179,132,149,181..., dimensions={0} | all-to-all | bytes 393216 | tf_op jit(solution)/shard_map/all_to_all | solution.py:273
  73.0 0.0 collective-permute-start.2
  73.0 1.2 early.7.refs_3_
  74.2 0.2 collective-permute-done.2.refs_0_.refs_3_.refs_1_.refs_4_
  74.4 0.6 late.7
  75.0 19.5 %all_to_all.33 = s32[128,1,384]{2,1,0:T(1,128)S(1)} all-to-all(s32[128,1,384]{2,1,0:T(1,128)S(1)} %bitcast.54), channel_id=1, replica_groups={{0,164,100,163,148,180,165,228,36,99,84,116,101,162,147,179,132,149,181..., dimensions={0} | all-to-all | bytes 393216 | tf_op jit(solution)/shard_map/all_to_all | solution.py:273
  94.6 0.0 collective-permute-start.3
  94.6 1.2 early.8.refs_3_
  95.8 0.2 collective-permute-done.3.refs_0_.refs_3_.refs_1_
  96.0 0.6 late.8
  96.6 19.4 %all_to_all.34 = s32[128,1,384]{2,1,0:T(1,128)S(1)} all-to-all(s32[128,1,384]{2,1,0:T(1,128)S(1)} %bitcast.55), channel_id=1, replica_groups={{0,164,100,163,148,180,165,228,36,99,84,116,101,162,147,179,132,149,181..., dimensions={0} | all-to-all | bytes 393216 | tf_op jit(solution)/shard_map/all_to_all | solution.py:273
  116.0 0.0 copy-start.4
  116.0 0.0 collective-permute-start.4
  116.0 1.2 early.9.refs_3_
  117.2 0.2 collective-permute-done.4.refs_0_
  117.4 0.7 late.9
  118.1 18.2 %all_to_all.35 = f32[256,1,128]{2,1,0:T(1,128)S(1)} all-to-all(f32[256,1,128]{2,1,0:T(1,128)S(1)} %bitcast.58), channel_id=1, replica_groups={{0,1,2,3,4,5,6,7,8,9,10,11,12,13,14,15,16,17,18,19,20,21,22,23,24,25,26..., dimensions={0} | all-to-all | bytes 262144 | tf_op jit(solution)/shard_map/all_to_all | solution.py:273
  136.3 0.0 copy-done.4
  136.3 0.8 rates.1
  (2 shorter events, 0.0 us)
Async XLA Ops:
  1.5 28.7 %copy-start = (bf16[1,128,128,128]{3,2,1,0:T(8,128)(2,1)S(1)}, bf16[1,128,128,128]{3,2,1,0:T(8,128)(2,1)}, u32[]{:S(2)}) copy-start(bf16[1,128,128,128]{3,2,1,0:T(8,128)(2,1)} %param.13) | copy-start | bytes 12582916
  1.6 29.7 %copy-start.1 = (f32[48,128]{1,0:T(8,128)S(1)}, f32[48,128]{1,0:T(8,128)}, u32[]{:S(2)}) copy-start(f32[48,128]{1,0:T(8,128)} %refs_3_.1) | copy-start | bytes 73732
  1.7 29.7 %copy-start.2 = (s32[128]{0:T(128)S(1)}, s32[128]{0:T(128)}, u32[]{:S(2)}) copy-start(s32[128]{0:T(128)} %param.11) | copy-start | bytes 1540
  1.7 29.7 %copy-start.3 = (s32[128]{0:T(128)S(1)}, s32[128]{0:T(128)}, u32[]{:S(2)}) copy-start(s32[128]{0:T(128)} %param.12) | copy-start | bytes 1540
  29.7 1.7 %collective-permute-start = (s32[384,128]{1,0:T(8,128)S(1)}, s32[384,128]{1,0:T(8,128)S(1)}, u32[]{:S(2)}, u32[]{:S(2)}) collective-permute-start(s32[384,128]{1,0:T(8,128)S(1)} %bitcast.34), channel_id=1, source_target_pairs={{0,8},{1,9},{2,10},{3,11},{4,12},{5,13},{6,14},{7,15},{8,0},{9,1},... | collective-permute-start | bytes 589832 | tf_op jit(solution)/shard_map/ppermute | solution.py:307
  51.6 1.4 %collective-permute-start.1 = (s32[384,128]{1,0:T(8,128)S(1)}, s32[384,128]{1,0:T(8,128)S(1)}, u32[]{:S(2)}, u32[]{:S(2)}) collective-permute-start(s32[384,128]{1,0:T(8,128)S(1)} %bitcast.39), channel_id=1, source_target_pairs={{0,8},{1,9},{2,10},{3,11},{4,12},{5,13},{6,14},{7,15},{8,0},{9,1},... | collective-permute-start | bytes 589832 | tf_op jit(solution)/shard_map/ppermute | solution.py:307
  73.0 1.4 %collective-permute-start.2 = (s32[384,128]{1,0:T(8,128)S(1)}, s32[384,128]{1,0:T(8,128)S(1)}, u32[]{:S(2)}, u32[]{:S(2)}) collective-permute-start(s32[384,128]{1,0:T(8,128)S(1)} %bitcast.43), channel_id=1, source_target_pairs={{0,8},{1,9},{2,10},{3,11},{4,12},{5,13},{6,14},{7,15},{8,0},{9,1},... | collective-permute-start | bytes 589832 | tf_op jit(solution)/shard_map/ppermute | solution.py:307
  94.6 1.4 %collective-permute-start.3 = (s32[384,128]{1,0:T(8,128)S(1)}, s32[384,128]{1,0:T(8,128)S(1)}, u32[]{:S(2)}, u32[]{:S(2)}) collective-permute-start(s32[384,128]{1,0:T(8,128)S(1)} %bitcast.47), channel_id=1, source_target_pairs={{0,8},{1,9},{2,10},{3,11},{4,12},{5,13},{6,14},{7,15},{8,0},{9,1},... | collective-permute-start | bytes 589832 | tf_op jit(solution)/shard_map/ppermute | solution.py:307
  116.0 20.3 %copy-start.4 = (s32[256,1]{0,1:T(1,128)S(1)}, s32[256,1]{0,1:T(1,128)}, u32[]{:S(2)}) copy-start(s32[256,1]{0,1:T(1,128)} %param.17) | copy-start | bytes 3076
  116.0 1.4 %collective-permute-start.4 = (s32[384,128]{1,0:T(8,128)S(1)}, s32[384,128]{1,0:T(8,128)S(1)}, u32[]{:S(2)}, u32[]{:S(2)}) collective-permute-start(s32[384,128]{1,0:T(8,128)S(1)} %bitcast.50), channel_id=1, source_target_pairs={{0,8},{1,9},{2,10},{3,11},{4,12},{5,13},{6,14},{7,15},{8,0},{9,1},... | collective-permute-start | bytes 589832 | tf_op jit(solution)/shard_map/ppermute | solution.py:307
